TPU v7x, 32 devices: a whole 2x2x4 slice. The times are simulated.
32 devices in a mesh: dp: 4 (over z), seq: 8 (over y, x, core).
Axes of the slice: x: 2, y: 2, z: 4, core: 2. Of those that a mesh axis runs over, the one named last changes fastest.
Arguments:
- queries: bfloat16 [4096, 64, 128], P(('dp', 'seq')), parts along dimension 0, may hold values from -52 to 52
- keys: bfloat16 [4096, 8, 128], P(('dp', 'seq')), parts along dimension 0, may hold values from -6 to 6
- values: bfloat16 [4096, 8, 128], P(('dp', 'seq')), parts along dimension 0, may hold values from -6 to 6
- doc_ids: int32 [4096], P(('dp', 'seq')), parts along dimension 0, may hold values from 0 to 7, never falling along the last dimension, each value on 1 to 512 neighbouring positions
- counts: int32 [32], P('dp'), parts along dimension 0, may hold values from 64 to 128
Outputs:
- attended: bfloat16 [4096, 64, 128], P(('dp', 'seq')), parts along dimension 0
There are 4 independent parts, one for each index of `dp`. A program takes and returns all parts, laid end to end along the dimension named above; each array names one. Nothing has to cross between parts.
Inputs may be any that keep to these rules, and one draw needn't show every extreme that they name: `doc_ids`: document numbers never fall along the sequence; each document has 1 to 512 positions. The first counts[j] positions of shard j are real tokens, the others padding.
All inputs are finite; a program needn't handle non-finite values.
Results may differ from a plain program's by a relative error of at most 0.003.
Values may be sent and summed in bfloat16 or wider, within the bound.
A program may use at most 64 MiB of HBM per device.

v0:
```python
import functools
import math

import jax
import jax.numpy as jnp
from jax import lax
from jax.experimental import pallas as pl
from jax.experimental.pallas import tpu as pltpu
from jax.sharding import PartitionSpec as P

DOC_MOST = 512
MESH = pl.DeviceIdType.MESH
NEG = -1e30


def kernel(
    n, reach, tile,
    counts_hbm, q_hbm, k_ref, v_ref, docs_hbm, out_ref,
    win, q_vmem, dwin, bias, counts_ref, small_sem,
    q_sem, send_sem, recv_sem, dsend_sem, drecv_sem,
):
    me = lax.axis_index("seq")
    heads, shard_rows, group, width = q_vmem.shape
    blocks = reach + 1
    keys_all = blocks * shard_rows
    rows = shard_rows * group
    tree = n == 8 and reach == 4

    def q_copy(h):
        return pltpu.make_async_copy(q_hbm.at[:, h], q_vmem.at[h], q_sem.at[h])

    def send(h, part, kind, from_off, to, to_off):
        source = (k_ref, v_ref)[part].at[h] if from_off == 0 else win.at[h, part, reach - from_off]
        return pltpu.make_async_remote_copy(
            src_ref=source,
            dst_ref=win.at[h, part, reach - to_off],
            send_sem=send_sem.at[h, part, kind],
            recv_sem=recv_sem.at[h, part, to_off - 1],
            device_id={"seq": to},
            device_id_type=MESH,
        )

    def send_docs(off):
        return pltpu.make_async_remote_copy(
            src_ref=dwin.at[reach],
            dst_ref=dwin.at[reach - off],
            send_sem=dsend_sem.at[off - 1],
            recv_sem=drecv_sem.at[off - 1],
            device_id={"seq": lax.rem(me + off, n)},
            device_id_type=MESH,
        )

    def wait_block(h, part, off):
        send(h, part, 0, 0, lax.rem(me + 1, n), off).wait_recv()

    def loop(body, count=None):
        lax.fori_loop(0, heads if count is None else count, lambda i, c: (body(i), c)[1], 0)

    doc_copy = pltpu.make_async_copy(docs_hbm, dwin.at[reach], small_sem.at[0])
    count_copy = pltpu.make_async_copy(counts_hbm, counts_ref, small_sem.at[1])
    doc_copy.start()
    count_copy.start()
    loop(lambda h: q_copy(h).start())

    barrier = pltpu.get_barrier_semaphore()
    for step in range(1, n):
        pl.semaphore_signal(
            barrier, inc=1, device_id={"seq": lax.rem(me + step, n)}, device_id_type=MESH
        )
    pl.semaphore_wait(barrier, n - 1)

    even = lax.rem(me, 2) == 0
    chip_odd = lax.rem(me // 2, 2) == 1
    if tree:
        own_sends = [
            (0, jnp.logical_not(chip_odd), 2),
            (1, me < 4, 4),
            (2, even, 1),
        ]
    else:
        own_sends = [(off - 1, me + off < n, off) for off in range(1, reach + 1)]

    def start_own(h):
        for kind, cond, off in own_sends:
            @pl.when(cond)
            def _(kind=kind, off=off):
                for part in range(2):
                    send(h, part, kind, 0, lax.rem(me + off, n), off).start()

    doc_copy.wait()
    count_copy.wait()
    for off in range(1, reach + 1):
        @pl.when(me + off < n)
        def _(off=off):
            send_docs(off).start()

    loop(start_own)

    def keep_own(h):
        win[h, 0, reach] = k_ref[h]
        win[h, 1, reach] = v_ref[h]

    loop(keep_own)

    for off in range(1, reach + 1):
        @pl.when(me < off)
        def _(off=off):
            dwin[reach - off] = jnp.full(dwin.shape[1:], -1, jnp.int32)

            def clear(h):
                win[h, :, reach - off] = jnp.zeros((2, shard_rows, width), win.dtype)

            loop(clear)

    for off in range(1, reach + 1):
        @pl.when(me >= off)
        def _(off=off):
            send_docs(off).wait_recv()

    lane = lax.broadcasted_iota(jnp.int32, (shard_rows, shard_rows), 1)
    row = lax.broadcasted_iota(jnp.int32, (shard_rows, shard_rows), 0)
    doc_col = jnp.transpose(jnp.broadcast_to(dwin[reach], (shard_rows, shard_rows)))
    for slot in range(blocks):
        off = reach - slot
        count = counts_ref[lax.max(me - off, 0)]
        docs = dwin[slot]
        allowed = (docs == doc_col) & (lane < count)
        if off == 0:
            allowed = allowed & (lane <= row)
        part = jnp.where(allowed, 0.0, NEG).astype(jnp.float32)
        part = jnp.broadcast_to(part[:, None, :], (shard_rows, group, shard_rows))
        bias[:, slot * shard_rows : (slot + 1) * shard_rows] = part.reshape(rows, shard_rows)

    own_count = counts_ref[me]
    factor = math.log2(math.e) / math.sqrt(width)

    def partner():
        return me + 1 - 2 * lax.rem(me, 2)

    def relay_two(h, part):
        wait_block(h, part, 2)

        @pl.when(even)
        def _():
            send(h, part, 3, 2, partner(), 3).start()

        @pl.when(jnp.logical_not(even))
        def _():
            send(h, part, 3, 2, partner(), 1).start()

    def relay_four(h, part):
        wait_block(h, part, 4)

        @pl.when(me >= 6)
        def _():
            send(h, part, 5, 4, me - 2, 2).start()

        @pl.when(jnp.logical_not(even))
        def _():
            send(h, part, 4, 4, me - 1, 3).start()

    def relay(h):
        for part in range(2):
            @pl.when(me >= 4)
            def _(part=part):
                relay_four(h, part)

            @pl.when(me >= 2)
            def _(part=part):
                relay_two(h, part)

    def attend(h):
        q_copy(h).wait()
        keys = win[h, 0].reshape(keys_all, width)
        values = win[h, 1].reshape(keys_all, width)

        def scores(start):
            q = q_vmem[h, start // group : (start + tile) // group].reshape(tile, width)
            return lax.dot_general(
                q, keys, (((1,), (1,)), ((), ())), preferred_element_type=jnp.float32
            )

        s_next = scores(0)
        for start in range(0, rows, tile):
            s = s_next
            if start + tile < rows:
                s_next = scores(start + tile)
            x = s * factor + bias[start : start + tile, :]
            top = jnp.max(x, axis=-1, keepdims=True)
            p = jnp.exp2(x - top)
            norm = jnp.sum(p, axis=-1, keepdims=True)
            o = lax.dot_general(
                p.astype(jnp.bfloat16), values, (((1,), (0,)), ((), ())),
                preferred_element_type=jnp.float32,
            )
            r = lax.broadcasted_iota(jnp.int32, (tile, width), 0) + start
            o = jnp.where(r < own_count * group, o / norm, 0.0).astype(jnp.bfloat16)
            out_ref[start // group : (start + tile) // group, h] = o.reshape(
                tile // group, group, width
            )

    def arrivals(h, offs):
        for off in offs:
            @pl.when(me >= off)
            def _(off=off):
                for part in range(2):
                    wait_block(h, part, off)

    def step(it):
        if tree:
            @pl.when(it < heads)
            def _():
                relay(it)

            @pl.when(it >= 1)
            def _():
                arrivals(it - 1, (1, 3))
                attend(it - 1)
        else:
            arrivals(it, range(1, reach + 1))
            attend(it)

    loop(step, heads + 1 if tree else heads)

    def finish(h):
        for part in range(2):
            for kind, cond, off in own_sends:
                @pl.when(cond)
                def _(part=part, kind=kind, off=off):
                    send(h, part, kind, 0, lax.rem(me + off, n), off).wait_send()
            if tree:
                @pl.when(me >= 2)
                def _(part=part):
                    send(h, part, 3, 2, partner(), 1).wait_send()

                @pl.when((me >= 4) & jnp.logical_not(even))
                def _(part=part):
                    send(h, part, 4, 4, me - 1, 3).wait_send()

                @pl.when(me >= 6)
                def _(part=part):
                    send(h, part, 5, 4, me - 2, 2).wait_send()

    loop(finish)
    for off in range(1, reach + 1):
        @pl.when(me + off < n)
        def _(off=off):
            send_docs(off).wait_send()


def local(n, queries, keys, values, doc_ids, counts):
    shard_rows, q_heads, width = queries.shape
    heads = keys.shape[1]
    group = q_heads // heads
    reach = min((DOC_MOST + shard_rows - 1) // shard_rows, n - 1)
    rows = shard_rows * group
    out = pl.pallas_call(
        functools.partial(kernel, n, reach, 256),
        out_shape=jax.ShapeDtypeStruct((shard_rows, heads, group, width), jnp.bfloat16),
        in_specs=[
            pl.BlockSpec(memory_space=pltpu.HBM),
            pl.BlockSpec(memory_space=pltpu.HBM),
            pl.BlockSpec(memory_space=pltpu.VMEM),
            pl.BlockSpec(memory_space=pltpu.VMEM),
            pl.BlockSpec(memory_space=pltpu.HBM),
        ],
        out_specs=pl.BlockSpec(memory_space=pltpu.VMEM),
        scratch_shapes=[
            pltpu.VMEM((heads, 2, reach + 1, shard_rows, width), jnp.bfloat16),
            pltpu.VMEM((heads, shard_rows, group, width), jnp.bfloat16),
            pltpu.VMEM((reach + 1, 1, shard_rows), jnp.int32),
            pltpu.VMEM((rows, (reach + 1) * shard_rows), jnp.float32),
            pltpu.SMEM(counts.shape, jnp.int32),
            pltpu.SemaphoreType.DMA((2,)),
            pltpu.SemaphoreType.DMA((heads,)),
            pltpu.SemaphoreType.DMA((heads, 2, 6)),
            pltpu.SemaphoreType.DMA((heads, 2, reach)),
            pltpu.SemaphoreType.DMA((reach,)),
            pltpu.SemaphoreType.DMA((reach,)),
        ],
        compiler_params=pltpu.CompilerParams(
            collective_id=0, has_side_effects=True, vmem_limit_bytes=51 << 20
        ),
    )(
        counts,
        queries.reshape(shard_rows, heads, group, width),
        jnp.transpose(keys, (1, 0, 2)),
        jnp.transpose(values, (1, 0, 2)),
        doc_ids.reshape(1, shard_rows),
    )
    return out.reshape(shard_rows, q_heads, width)


def solution(mesh):
    in_specs = (
        P(("dp", "seq"), None, None),
        P(("dp", "seq"), None, None),
        P(("dp", "seq"), None, None),
        P(("dp", "seq")),
        P("dp"),
    )
    out_specs = P(("dp", "seq"), None, None)
    return jax.shard_map(
        functools.partial(local, mesh.shape["seq"]),
        mesh=mesh, in_specs=in_specs, out_specs=out_specs, check_vma=False,
    )
```

profile of v0, /device:TPU:13, one launch (start us, length us, event | category | flops | bytes accessed | tf_op | source)
XLA Modules:
  0.0 26.8 jit_solution(12404693588752868677)
XLA Ops:
  0.0 1.1 %copy_bitcast_fusion = (bf16[8,128,128]{2,1,0:T(8,128)(2,1)S(1)}, bf16[8,128,128]{2,1,0:T(8,128)(2,1)S(1)}) fusion(bf16[128,8,128]{2,1,0:T(8,128)(2,1)} %param.7, bf16[128,8,128]{2,1,0:T(8,128)(2,1)} %param.6), kind=kLoop, calls=%fused_computation | loop fusion | bytes 1048576 | tf_op jit(solution)/shard_map/transpose | solution.py:288
  1.1 0.0 copy-start
  1.1 0.6 %copy-done = s32[8]{0:T(128)S(1)} copy-done((s32[8]{0:T(128)S(1)}, s32[8]{0:T(128)}, u32[]{:S(2)}) %copy-start) | copy-done | bytes 56
  1.8 0.0 copy-start.1
  1.8 0.7 %copy-done.1 = s32[128]{0:T(128)S(1)} copy-done((s32[128]{0:T(128)S(1)}, s32[128]{0:T(128)}, u32[]{:S(2)}) %copy-start.1) | copy-done | bytes 536
  2.4 23.0 %shard_map.55 = bf16[128,8,8,128]{3,2,1,0:T(8,128)(2,1)S(1)} custom-call(s32[8]{0:T(128)S(1)} %copy-done, bf16[128,8,8,128]{3,2,1,0:T(8,128)(2,1)} %bitcast.9, bf16[8,128,128]{2,1,0:T(8,128)(2,1)S(1)} %get-tuple-element.6.k_ref, bf16[8,128,128]{2,1,0:T(8,128)(2,1)S(1)} %get-tuple-element.5.v_ref, s32[1,128]{1,0:T(1,128)S(1)} %bitcast.8), custom_call_target="tpu_custom_call" | custom-call | tf_op jit(solution)/shard_map/pallas_call | solution.py:257
  25.4 1.3 %copy.11 = bf16[128,64,128]{2,1,0:T(8,128)(2,1)} copy(bf16[128,64,128]{2,1,0:T(8,128)(2,1)S(1)} %bitcast.7) | data formatting | bytes 4194304
Async XLA Ops:
  1.1 0.7 %copy-start = (s32[8]{0:T(128)S(1)}, s32[8]{0:T(128)}, u32[]{:S(2)}) copy-start(s32[8]{0:T(128)} %counts_hbm.1) | copy-start | bytes 100
  1.8 0.7 %copy-start.1 = (s32[128]{0:T(128)S(1)}, s32[128]{0:T(128)}, u32[]{:S(2)}) copy-start(s32[128]{0:T(128)} %param.8) | copy-start | bytes 1540
where the time goes:
time: 26.9 us; the launch traced here: 26.8 us
  Pallas kernels  23 us (86%)
  local copies, waits for them, and re-layouts  3.75 us (14%)
    pallas_call x1, Pallas kernels, local(): pl.pallas_call(functools.partial(kernel, n, reach, 256), out_shape=jax.Sh...  23 us
    unnamed x5, local copies, waits for them, and re-layouts  2.63 us
    transpose x1, local copies, waits for them, and re-layouts, local(): jnp.transpose(values, (1, 0, 2))  1.12 us

commit v1 on v0

v1 whole, which is shorter than its diff:
```python
import functools
import math

import jax
import jax.numpy as jnp
from jax import lax
from jax.experimental import pallas as pl
from jax.experimental.pallas import tpu as pltpu
from jax.sharding import PartitionSpec as P

DOC_MOST = 512
MESH = pl.DeviceIdType.MESH
NEG = -1e30


def kernel(
    n, reach, tile,
    counts_hbm, q_hbm, k_hbm, v_hbm, docs_hbm, out_ref,
    raw, win, q_vmem, dwin, bias, counts_ref, small_sem, raw_sem,
    q_sem, send_sem, recv_sem, dsend_sem, drecv_sem,
):
    me = lax.axis_index("seq")
    heads, shard_rows, group, width = q_vmem.shape
    blocks = reach + 1
    keys_all = blocks * shard_rows
    rows = shard_rows * group
    tree = n == 8 and reach == 4

    even = lax.rem(me, 2) == 0
    odd = jnp.logical_not(even)
    chip_odd = lax.rem(me // 2, 2) == 1
    partner = me + 1 - 2 * lax.rem(me, 2)
    if tree:
        own_sends = [
            (0, jnp.logical_not(chip_odd), 2),
            (1, me < 4, 4),
            (2, even, 1),
        ]
        senders = [
            (odd | (me >= 2), partner),
            (chip_odd, me - 2),
            (me >= 4, me - 4),
            ((me >= 4) & (me < 6), me + 2),
        ]
        targets = [even | (me >= 2), jnp.logical_not(chip_odd), me < 4, me >= 6]
    else:
        own_sends = [(off - 1, me + off < n, off) for off in range(1, reach + 1)]
        senders = [(me >= off, me - off) for off in range(1, reach + 1)]
        targets = [me + off < n for off in range(1, reach + 1)]

    barrier = pltpu.get_barrier_semaphore()
    for cond, device in senders:
        @pl.when(cond)
        def _(device=device):
            pl.semaphore_signal(
                barrier, inc=1, device_id={"seq": lax.rem(device + n, n)},
                device_id_type=MESH,
            )

    def loop(body, count=None):
        lax.fori_loop(0, heads if count is None else count, lambda i, c: (body(i), c)[1], 0)

    raw_copies = [
        pltpu.make_async_copy(ref, raw.at[part], raw_sem.at[part])
        for part, ref in enumerate((k_hbm, v_hbm))
    ]
    doc_copy = pltpu.make_async_copy(docs_hbm, dwin.at[reach], small_sem.at[0])
    count_copy = pltpu.make_async_copy(counts_hbm, counts_ref, small_sem.at[1])
    doc_copy.start()
    for copy in raw_copies:
        copy.start()
    count_copy.start()

    def q_copy(h):
        return pltpu.make_async_copy(q_hbm.at[:, h], q_vmem.at[h], q_sem.at[h])

    def send(item, kind, from_off, to, to_off):
        if item is None:
            src, dst = dwin.at[reach - from_off], dwin.at[reach - to_off]
            sems = dsend_sem.at[kind], drecv_sem.at[to_off - 1]
        else:
            h, part = item
            src, dst = win.at[h, part, reach - from_off], win.at[h, part, reach - to_off]
            sems = send_sem.at[h, part, kind], recv_sem.at[h, part, to_off - 1]
        return pltpu.make_async_remote_copy(
            src_ref=src, dst_ref=dst, send_sem=sems[0], recv_sem=sems[1],
            device_id={"seq": to}, device_id_type=MESH,
        )

    def wait_block(item, off):
        send(item, 0, 0, lax.rem(me + 1, n), off).wait_recv()

    def start_own(item):
        for kind, cond, off in own_sends:
            @pl.when(cond)
            def _(kind=kind, off=off):
                send(item, kind, 0, lax.rem(me + off, n), off).start()

    doc_copy.wait()
    for part in range(2):
        raw_copies[part].wait()
        win[:, part, reach] = jnp.swapaxes(raw[part], 0, 1)
    pl.semaphore_wait(barrier, sum(jnp.where(cond, 1, 0) for cond in targets))

    start_own(None)

    def start_head(h):
        for part in range(2):
            start_own((h, part))

    loop(start_head)
    loop(lambda h: q_copy(h).start())
    count_copy.wait()

    for off in range(1, reach + 1):
        @pl.when(me < off)
        def _(off=off):
            dwin[reach - off] = jnp.full(dwin.shape[1:], -1, jnp.int32)

            def clear(h):
                win[h, :, reach - off] = jnp.zeros((2, shard_rows, width), win.dtype)

            loop(clear)

    def relay_two(item):
        wait_block(item, 2)

        @pl.when(even)
        def _():
            send(item, 3, 2, partner, 3).start()

        @pl.when(odd)
        def _():
            send(item, 3, 2, partner, 1).start()

    def relay_four(item):
        wait_block(item, 4)

        @pl.when(me >= 6)
        def _():
            send(item, 5, 4, me - 2, 2).start()

        @pl.when(odd)
        def _():
            send(item, 4, 4, me - 1, 3).start()

    def relay(item):
        @pl.when(me >= 4)
        def _():
            relay_four(item)

        @pl.when(me >= 2)
        def _():
            relay_two(item)

    def arrivals(item, offs):
        for off in offs:
            @pl.when(me >= off)
            def _(off=off):
                wait_block(item, off)

    if tree:
        relay(None)
        arrivals(None, (1, 3))
    else:
        arrivals(None, range(1, reach + 1))

    lane = lax.broadcasted_iota(jnp.int32, (shard_rows, shard_rows), 1)
    row = lax.broadcasted_iota(jnp.int32, (shard_rows, shard_rows), 0)
    doc_col = jnp.transpose(jnp.broadcast_to(dwin[reach], (shard_rows, shard_rows)))
    for slot in range(blocks):
        off = reach - slot
        count = counts_ref[lax.max(me - off, 0)]
        docs = dwin[slot]
        allowed = (docs == doc_col) & (lane < count)
        if off == 0:
            allowed = allowed & (lane <= row)
        part = jnp.where(allowed, 0.0, NEG).astype(jnp.float32)
        part = jnp.broadcast_to(part[:, None, :], (shard_rows, group, shard_rows))
        bias[:, slot * shard_rows : (slot + 1) * shard_rows] = part.reshape(rows, shard_rows)

    own_count = counts_ref[me]
    factor = math.log2(math.e) / math.sqrt(width)

    def attend(h):
        q_copy(h).wait()
        keys = win[h, 0].reshape(keys_all, width)
        values = win[h, 1].reshape(keys_all, width)

        def scores(start):
            q = q_vmem[h, start // group : (start + tile) // group].reshape(tile, width)
            return lax.dot_general(
                q, keys, (((1,), (1,)), ((), ())), preferred_element_type=jnp.float32
            )

        s_next = scores(0)
        for start in range(0, rows, tile):
            s = s_next
            if start + tile < rows:
                s_next = scores(start + tile)
            x = s * factor + bias[start : start + tile, :]
            top = jnp.max(x, axis=-1, keepdims=True)
            p = jnp.exp2(x - top)
            norm = jnp.sum(p, axis=-1, keepdims=True)
            o = lax.dot_general(
                p.astype(jnp.bfloat16), values, (((1,), (0,)), ((), ())),
                preferred_element_type=jnp.float32,
            )
            r = lax.broadcasted_iota(jnp.int32, (tile, width), 0) + start
            o = jnp.where(r < own_count * group, o / norm, 0.0).astype(jnp.bfloat16)
            out_ref[start // group : (start + tile) // group, h] = o.reshape(
                tile // group, group, width
            )

    def step(it):
        if tree:
            @pl.when(it < heads)
            def _():
                for part in range(2):
                    relay((it, part))

            @pl.when(it >= 1)
            def _():
                for part in range(2):
                    arrivals((it - 1, part), (1, 3))
                attend(it - 1)
        else:
            for part in range(2):
                arrivals((it, part), range(1, reach + 1))
            attend(it)

    loop(step, heads + 1 if tree else heads)

    def finish(item):
        for kind, cond, off in own_sends:
            @pl.when(cond)
            def _(kind=kind, off=off):
                send(item, kind, 0, lax.rem(me + off, n), off).wait_send()
        if tree:
            @pl.when(me >= 2)
            def _():
                send(item, 3, 2, partner, 1).wait_send()

            @pl.when((me >= 4) & odd)
            def _():
                send(item, 4, 4, me - 1, 3).wait_send()

            @pl.when(me >= 6)
            def _():
                send(item, 5, 4, me - 2, 2).wait_send()

    finish(None)

    def finish_head(h):
        for part in range(2):
            finish((h, part))

    loop(finish_head)


def local(n, queries, keys, values, doc_ids, counts):
    shard_rows, q_heads, width = queries.shape
    heads = keys.shape[1]
    group = q_heads // heads
    reach = min((DOC_MOST + shard_rows - 1) // shard_rows, n - 1)
    rows = shard_rows * group
    out = pl.pallas_call(
        functools.partial(kernel, n, reach, 512),
        out_shape=pltpu.VMEM((shard_rows, heads, group, width), jnp.bfloat16),
        in_specs=[pl.BlockSpec(memory_space=pltpu.HBM)] * 5,
        out_specs=pl.BlockSpec(memory_space=pltpu.VMEM),
        scratch_shapes=[
            pltpu.VMEM((2, shard_rows, heads, width), jnp.bfloat16),
            pltpu.VMEM((heads, 2, reach + 1, shard_rows, width), jnp.bfloat16),
            pltpu.VMEM((heads, shard_rows, group, width), jnp.bfloat16),
            pltpu.VMEM((reach + 1, 1, shard_rows), jnp.int32),
            pltpu.VMEM((rows, (reach + 1) * shard_rows), jnp.float32),
            pltpu.SMEM(counts.shape, jnp.int32),
            pltpu.SemaphoreType.DMA((2,)),
            pltpu.SemaphoreType.DMA((2,)),
            pltpu.SemaphoreType.DMA((heads,)),
            pltpu.SemaphoreType.DMA((heads, 2, 6)),
            pltpu.SemaphoreType.DMA((heads, 2, reach)),
            pltpu.SemaphoreType.DMA((6,)),
            pltpu.SemaphoreType.DMA((reach,)),
        ],
        compiler_params=pltpu.CompilerParams(
            collective_id=0, has_side_effects=True, vmem_limit_bytes=51 << 20
        ),
    )(
        *(
            pltpu.with_memory_space_constraint(x, pltpu.HBM)
            for x in (
                counts,
                queries.reshape(shard_rows, heads, group, width),
                keys,
                values,
                doc_ids.reshape(1, shard_rows),
            )
        )
    )
    return out.reshape(shard_rows, q_heads, width)


def solution(mesh):
    in_specs = (
        P(("dp", "seq"), None, None),
        P(("dp", "seq"), None, None),
        P(("dp", "seq"), None, None),
        P(("dp", "seq")),
        P("dp"),
    )
    out_specs = P(("dp", "seq"), None, None)
    return jax.shard_map(
        functools.partial(local, mesh.shape["seq"]),
        mesh=mesh, in_specs=in_specs, out_specs=out_specs, check_vma=False,
    )
```

time: 26.9 us -> 24.7 us (0.918)
  local copies, waits for them, and re-layouts: 3.75 us -> 1.32 us
    unnamed x5 -> x1, local copies, waits for them, and re-layouts: 2.63 us -> 1.32 us
    transpose x1 -> x0, local copies, waits for them, and re-layouts: 1.12 us -> none  [local(): jnp.transpose(values, (1, 0, 2))]
where the time goes in v1:
time: 24.7 us; the launch traced here: 24.5 us
  Pallas kernels  23.2 us (94%)
  local copies, waits for them, and re-layouts  1.32 us (5%)
    pallas_call x1, Pallas kernels, local(): pl.pallas_call(functools.partial(kernel, n, reach, 512), out_shape=pltpu....  23.2 us
    unnamed x1, local copies, waits for them, and re-layouts  1.32 us

profile of v1, /device:TPU:13, one launch (start us, length us, event | category | flops | bytes accessed | tf_op | source)
XLA Modules:
  0.0 24.5 jit_solution(6882196458274240821)
XLA Ops:
  0.0 23.2 %shard_map.55 = bf16[128,8,8,128]{3,2,1,0:T(8,128)(2,1)S(1)} custom-call(s32[8]{0:T(128)} %counts_hbm.1, bf16[128,8,8,128]{3,2,1,0:T(8,128)(2,1)} %bitcast.4, bf16[128,8,128]{2,1,0:T(8,128)(2,1)} %k_hbm.1, bf16[128,8,128]{2,1,0:T(8,128)(2,1)} %v_hbm.1, s32[1,128]{1,0:T(1,128)} %bitcast.5), custom_call_target="tpu_custom_call" | custom-call | tf_op jit(solution)/shard_map/pallas_call | solution.py:267
  23.2 1.3 %copy.7 = bf16[128,64,128]{2,1,0:T(8,128)(2,1)} copy(bf16[128,64,128]{2,1,0:T(8,128)(2,1)S(1)} %bitcast.3) | data formatting | bytes 4194304

commit v2 on v1

--- a/solution.py
+++ b/solution.py
@@ -16,13 +16,12 @@
 def kernel(
     n, reach, tile,
     counts_hbm, q_hbm, k_hbm, v_hbm, docs_hbm, out_ref,
-    raw, win, q_vmem, dwin, bias, counts_ref, small_sem, raw_sem,
+    raw, win, q_vmem, dwin, bias, top_ref, norm_ref, part_ref, counts_ref, small_sem, raw_sem,
     q_sem, send_sem, recv_sem, dsend_sem, drecv_sem,
 ):
     me = lax.axis_index("seq")
     heads, shard_rows, group, width = q_vmem.shape
     blocks = reach + 1
-    keys_all = blocks * shard_rows
     rows = shard_rows * group
     tree = n == 8 and reach == 4
 
@@ -38,15 +37,19 @@
         ]
         senders = [
             (odd | (me >= 2), partner),
-            (chip_odd, me - 2),
+            (chip_odd | (me == 4) | (me == 5), me - 2),
             (me >= 4, me - 4),
             ((me >= 4) & (me < 6), me + 2),
         ]
-        targets = [even | (me >= 2), jnp.logical_not(chip_odd), me < 4, me >= 6]
+        targets = [even | (me >= 2), (me < 4) | jnp.logical_not(chip_odd), me < 4, me >= 6]
+        straight = (me == 2) | (me == 3)
+        send_shift = jnp.where(me >= 2, 1, 0)
+        shift = jnp.where(me >= 6, 1, 0)
     else:
         own_sends = [(off - 1, me + off < n, off) for off in range(1, reach + 1)]
         senders = [(me >= off, me - off) for off in range(1, reach + 1)]
         targets = [me + off < n for off in range(1, reach + 1)]
+        send_shift = shift = 0
 
     barrier = pltpu.get_barrier_semaphore()
     for cond, device in senders:
@@ -73,6 +76,8 @@
 
     def q_copy(h):
         return pltpu.make_async_copy(q_hbm.at[:, h], q_vmem.at[h], q_sem.at[h])
+
+    loop(lambda h: q_copy(h).start())
 
     def send(item, kind, from_off, to, to_off):
         if item is None:
@@ -103,13 +108,17 @@
     pl.semaphore_wait(barrier, sum(jnp.where(cond, 1, 0) for cond in targets))
 
     start_own(None)
-
-    def start_head(h):
+    if tree:
+        @pl.when(straight)
+        def _():
+            for item in (None, (0, 0), (0, 1)):
+                send(item, 6, 0, me + 2, 2).start()
+
+    def start_head(i):
         for part in range(2):
-            start_own((h, part))
+            start_own((lax.rem(i + send_shift, heads), part))
 
     loop(start_head)
-    loop(lambda h: q_copy(h).start())
     count_copy.wait()
 
     for off in range(1, reach + 1):
@@ -136,9 +145,10 @@
     def relay_four(item):
         wait_block(item, 4)
 
-        @pl.when(me >= 6)
-        def _():
-            send(item, 5, 4, me - 2, 2).start()
+        if item is not None:
+            @pl.when((me >= 6) & (item[0] > 0))
+            def _():
+                send(item, 5, 4, me - 2, 2).start()
 
         @pl.when(odd)
         def _():
@@ -159,16 +169,11 @@
             def _(off=off):
                 wait_block(item, off)
 
-    if tree:
-        relay(None)
-        arrivals(None, (1, 3))
-    else:
-        arrivals(None, range(1, reach + 1))
-
     lane = lax.broadcasted_iota(jnp.int32, (shard_rows, shard_rows), 1)
     row = lax.broadcasted_iota(jnp.int32, (shard_rows, shard_rows), 0)
     doc_col = jnp.transpose(jnp.broadcast_to(dwin[reach], (shard_rows, shard_rows)))
-    for slot in range(blocks):
+
+    def fill_bias(slot):
         off = reach - slot
         count = counts_ref[lax.max(me - off, 0)]
         docs = dwin[slot]
@@ -181,55 +186,108 @@
 
     own_count = counts_ref[me]
     factor = math.log2(math.e) / math.sqrt(width)
+    remote = reach * shard_rows
+    together = math.gcd(heads, 4)
+
+    def scores(h, start, keys):
+        q = q_vmem[h, start // group : (start + tile) // group].reshape(tile, width)
+        return lax.dot_general(
+            q, keys, (((1,), (1,)), ((), ())), preferred_element_type=jnp.float32
+        )
+
+    def mix(p, values):
+        return lax.dot_general(
+            p.astype(jnp.bfloat16), values, (((1,), (0,)), ((), ())),
+            preferred_element_type=jnp.float32,
+        )
+
+    def own_scores(h):
+        q_copy(h).wait()
+        q = q_vmem[h].reshape(rows, width)
+        return lax.dot_general(
+            q, win[h, 0, reach], (((1,), (1,)), ((), ())), preferred_element_type=jnp.float32
+        )
+
+    def own_weights(h, s):
+        x = s * factor + bias[:, remote:]
+        top = jnp.max(x, axis=-1, keepdims=True)
+        top_ref[h] = jnp.broadcast_to(top, (rows, width))
+        return jnp.exp2(x - top)
+
+    def own_mix(h, p):
+        ones = jnp.ones((shard_rows, width), jnp.bfloat16)
+        o = mix(p, jnp.concatenate([win[h, 1, reach], ones], axis=1))
+        part_ref[h] = o[:, :width]
+        norm_ref[h] = o[:, width:]
+
+    def attend_own(i):
+        hs = [i * together + u for u in range(together)]
+        s, p = {}, {}
+        for k in range(together + 2):
+            if k < together:
+                s[k] = own_scores(hs[k])
+            if 1 <= k <= together:
+                p[k - 1] = own_weights(hs[k - 1], s.pop(k - 1))
+            if k >= 2:
+                own_mix(hs[k - 2], p.pop(k - 2))
 
     def attend(h):
-        q_copy(h).wait()
-        keys = win[h, 0].reshape(keys_all, width)
-        values = win[h, 1].reshape(keys_all, width)
-
-        def scores(start):
-            q = q_vmem[h, start // group : (start + tile) // group].reshape(tile, width)
-            return lax.dot_general(
-                q, keys, (((1,), (1,)), ((), ())), preferred_element_type=jnp.float32
-            )
-
-        s_next = scores(0)
+        keys = win[h, 0, :reach].reshape(remote, width)
+        values = win[h, 1, :reach].reshape(remote, width)
+        s_next = scores(h, 0, keys)
         for start in range(0, rows, tile):
+            at = slice(start, start + tile)
             s = s_next
             if start + tile < rows:
-                s_next = scores(start + tile)
-            x = s * factor + bias[start : start + tile, :]
-            top = jnp.max(x, axis=-1, keepdims=True)
-            p = jnp.exp2(x - top)
-            norm = jnp.sum(p, axis=-1, keepdims=True)
-            o = lax.dot_general(
-                p.astype(jnp.bfloat16), values, (((1,), (0,)), ((), ())),
-                preferred_element_type=jnp.float32,
-            )
+                s_next = scores(h, start + tile, keys)
+            x = s * factor + bias[at, :remote]
+            own_top = top_ref[h, at]
+            top = jnp.maximum(jnp.max(x, axis=-1, keepdims=True), own_top)
+            p = jnp.exp2(x - jnp.concatenate([top] * reach, axis=1))
+            own = jnp.exp2(own_top - top)
+            norm = jnp.sum(p, axis=-1, keepdims=True) + own * norm_ref[h, at]
+            o = mix(p, values) + own * part_ref[h, at]
             r = lax.broadcasted_iota(jnp.int32, (tile, width), 0) + start
             o = jnp.where(r < own_count * group, o / norm, 0.0).astype(jnp.bfloat16)
             out_ref[start // group : (start + tile) // group, h] = o.reshape(
                 tile // group, group, width
             )
 
-    def step(it):
+    def order(i):
+        return lax.rem(i + shift, heads)
+
+    def relay_head(h):
+        for part in range(2):
+            relay((h, part))
+
+    batches = heads // together
+
+    def prepare(i):
+        attend_own(i)
         if tree:
-            @pl.when(it < heads)
-            def _():
-                for part in range(2):
-                    relay((it, part))
-
-            @pl.when(it >= 1)
-            def _():
-                for part in range(2):
-                    arrivals((it - 1, part), (1, 3))
-                attend(it - 1)
-        else:
-            for part in range(2):
-                arrivals((it, part), range(1, reach + 1))
-            attend(it)
-
-    loop(step, heads + 1 if tree else heads)
+            @pl.when(i == jnp.where(me >= 6, 0, batches - 1))
+            def _():
+                relay(None)
+                relay_head(order(0))
+
+    fill_bias(reach)
+    loop(prepare, batches)
+    arrivals(None, (1, 3) if tree else range(1, reach + 1))
+    for slot in range(reach):
+        fill_bias(slot)
+
+    def step(i):
+        h = order(i)
+        if tree:
+            @pl.when(i + 1 < heads)
+            def _():
+                relay_head(order(i + 1))
+
+        for part in range(2):
+            arrivals((h, part), (1, 3) if tree else range(1, reach + 1))
+        attend(h)
+
+    loop(step)
 
     def finish(item):
         for kind, cond, off in own_sends:
@@ -245,11 +303,17 @@
             def _():
                 send(item, 4, 4, me - 1, 3).wait_send()
 
-            @pl.when(me >= 6)
-            def _():
-                send(item, 5, 4, me - 2, 2).wait_send()
+            if item is not None:
+                @pl.when((me >= 6) & (item[0] > 0))
+                def _():
+                    send(item, 5, 4, me - 2, 2).wait_send()
 
     finish(None)
+    if tree:
+        @pl.when(straight)
+        def _():
+            for item in (None, (0, 0), (0, 1)):
+                send(item, 6, 0, me + 2, 2).wait_send()
 
     def finish_head(h):
         for part in range(2):
@@ -275,13 +339,16 @@
             pltpu.VMEM((heads, shard_rows, group, width), jnp.bfloat16),
             pltpu.VMEM((reach + 1, 1, shard_rows), jnp.int32),
             pltpu.VMEM((rows, (reach + 1) * shard_rows), jnp.float32),
+            pltpu.VMEM((heads, rows, width), jnp.float32),
+            pltpu.VMEM((heads, rows, width), jnp.float32),
+            pltpu.VMEM((heads, rows, width), jnp.float32),
             pltpu.SMEM(counts.shape, jnp.int32),
             pltpu.SemaphoreType.DMA((2,)),
             pltpu.SemaphoreType.DMA((2,)),
             pltpu.SemaphoreType.DMA((heads,)),
-            pltpu.SemaphoreType.DMA((heads, 2, 6)),
+            pltpu.SemaphoreType.DMA((heads, 2, 7)),
             pltpu.SemaphoreType.DMA((heads, 2, reach)),
-            pltpu.SemaphoreType.DMA((6,)),
+            pltpu.SemaphoreType.DMA((7,)),
             pltpu.SemaphoreType.DMA((reach,)),
         ],
         compiler_params=pltpu.CompilerParams(

time: 24.7 us -> 23.5 us (0.951)
  Pallas kernels: 23.2 us -> 22 us
    pallas_call x1, Pallas kernels: 23.2 us -> 22 us  [local(): pl.pallas_call(functools.partial(kernel, n, reach, 512), out_shape=pltpu....]
where the time goes in v2:
time: 23.5 us; the launch traced here: 23.4 us
  Pallas kernels  22 us (94%)
  local copies, waits for them, and re-layouts  1.32 us (6%)
    pallas_call x1, Pallas kernels, local(): pl.pallas_call(functools.partial(kernel, n, reach, 512), out_shape=pltpu....  22 us
    unnamed x1, local copies, waits for them, and re-layouts  1.32 us

profile of v2, /device:TPU:13, one launch (start us, length us, event | category | flops | bytes accessed | tf_op | source)
XLA Modules:
  0.0 23.4 jit_solution(6916931341932177299)
XLA Ops:
  0.0 22.0 %shard_map.55 = bf16[128,8,8,128]{3,2,1,0:T(8,128)(2,1)S(1)} custom-call(s32[8]{0:T(128)} %counts_hbm.1, bf16[128,8,8,128]{3,2,1,0:T(8,128)(2,1)} %bitcast.4, bf16[128,8,128]{2,1,0:T(8,128)(2,1)} %k_hbm.1, bf16[128,8,128]{2,1,0:T(8,128)(2,1)} %v_hbm.1, s32[1,128]{1,0:T(1,128)} %bitcast.5), custom_call_target="tpu_custom_call" | custom-call | tf_op jit(solution)/shard_map/pallas_call | solution.py:331
  22.0 1.3 %copy.7 = bf16[128,64,128]{2,1,0:T(8,128)(2,1)} copy(bf16[128,64,128]{2,1,0:T(8,128)(2,1)S(1)} %bitcast.3) | data formatting | bytes 4194304

commit v3 on v2

--- a/solution.py
+++ b/solution.py
@@ -21,7 +21,7 @@
 ):
     me = lax.axis_index("seq")
     heads, shard_rows, group, width = q_vmem.shape
-    blocks = reach + 1
+    together = math.gcd(heads, 4)
     rows = shard_rows * group
     tree = n == 8 and reach == 4
 
@@ -75,9 +75,14 @@
     count_copy.start()
 
     def q_copy(h):
-        return pltpu.make_async_copy(q_hbm.at[:, h], q_vmem.at[h], q_sem.at[h])
+        return pltpu.make_async_copy(q_hbm.at[:, h], q_vmem.at[h], q_sem.at[h // together])
 
     loop(lambda h: q_copy(h).start())
+
+    def recv_index(part, off):
+        if not tree:
+            return off - 1
+        return {1: 3, 2: 0, 3: 3, 4: 1 + part}[off]
 
     def send(item, kind, from_off, to, to_off):
         if item is None:
@@ -86,14 +91,23 @@
         else:
             h, part = item
             src, dst = win.at[h, part, reach - from_off], win.at[h, part, reach - to_off]
-            sems = send_sem.at[h, part, kind], recv_sem.at[h, part, to_off - 1]
+            sems = send_sem.at[kind], recv_sem.at[h, recv_index(part, to_off)]
         return pltpu.make_async_remote_copy(
             src_ref=src, dst_ref=dst, send_sem=sems[0], recv_sem=sems[1],
             device_id={"seq": to}, device_id_type=MESH,
         )
 
+    def many(ref, kind=0, recv=(0, 0)):
+        return pltpu.make_async_remote_copy(
+            src_ref=ref, dst_ref=ref, send_sem=send_sem.at[kind], recv_sem=recv_sem.at[recv],
+            device_id={"seq": lax.rem(me + 1, n)}, device_id_type=MESH,
+        )
+
     def wait_block(item, off):
         send(item, 0, 0, lax.rem(me + 1, n), off).wait_recv()
+
+    def wait_both(h, off):
+        many(win.at[h, :, reach - off], recv=(h, recv_index(0, off))).wait_recv()
 
     def start_own(item):
         for kind, cond, off in own_sends:
@@ -131,16 +145,20 @@
 
             loop(clear)
 
-    def relay_two(item):
-        wait_block(item, 2)
-
-        @pl.when(even)
-        def _():
-            send(item, 3, 2, partner, 3).start()
-
-        @pl.when(odd)
-        def _():
-            send(item, 3, 2, partner, 1).start()
+    def relay_two(h):
+        if h is None:
+            wait_block(None, 2)
+        else:
+            wait_both(h, 2)
+
+        for item in [None] if h is None else [(h, 0), (h, 1)]:
+            @pl.when(even)
+            def _(item=item):
+                send(item, 3, 2, partner, 3).start()
+
+            @pl.when(odd)
+            def _(item=item):
+                send(item, 3, 2, partner, 1).start()
 
     def relay_four(item):
         wait_block(item, 4)
@@ -154,20 +172,35 @@
         def _():
             send(item, 4, 4, me - 1, 3).start()
 
-    def relay(item):
+    def relay(h):
         @pl.when(me >= 4)
         def _():
-            relay_four(item)
+            for item in [None] if h is None else [(h, 0), (h, 1)]:
+                relay_four(item)
 
         @pl.when(me >= 2)
         def _():
-            relay_two(item)
-
-    def arrivals(item, offs):
-        for off in offs:
-            @pl.when(me >= off)
-            def _(off=off):
-                wait_block(item, off)
+            relay_two(h)
+
+    def arrivals(h):
+        if h is None:
+            for off in (1, 3) if tree else range(1, reach + 1):
+                @pl.when(me >= off)
+                def _(off=off):
+                    wait_block(None, off)
+        elif tree:
+            @pl.when(me >= 3)
+            def _():
+                many(win.at[h, :, :2], recv=(h, 3)).wait_recv()
+
+            @pl.when((me == 1) | (me == 2))
+            def _():
+                many(win.at[h, :, 0], recv=(h, 3)).wait_recv()
+        else:
+            for off in range(1, reach + 1):
+                @pl.when(me >= off)
+                def _(off=off):
+                    wait_both(h, off)
 
     lane = lax.broadcasted_iota(jnp.int32, (shard_rows, shard_rows), 1)
     row = lax.broadcasted_iota(jnp.int32, (shard_rows, shard_rows), 0)
@@ -187,7 +220,6 @@
     own_count = counts_ref[me]
     factor = math.log2(math.e) / math.sqrt(width)
     remote = reach * shard_rows
-    together = math.gcd(heads, 4)
 
     def scores(h, start, keys):
         q = q_vmem[h, start // group : (start + tile) // group].reshape(tile, width)
@@ -202,7 +234,6 @@
         )
 
     def own_scores(h):
-        q_copy(h).wait()
         q = q_vmem[h].reshape(rows, width)
         return lax.dot_general(
             q, win[h, 0, reach], (((1,), (1,)), ((), ())), preferred_element_type=jnp.float32
@@ -222,6 +253,8 @@
 
     def attend_own(i):
         hs = [i * together + u for u in range(together)]
+        all_q = q_vmem.at[pl.ds(i * together, together)]
+        pltpu.make_async_copy(all_q, all_q, q_sem.at[i]).wait()
         s, p = {}, {}
         for k in range(together + 2):
             if k < together:
@@ -256,10 +289,6 @@
     def order(i):
         return lax.rem(i + shift, heads)
 
-    def relay_head(h):
-        for part in range(2):
-            relay((h, part))
-
     batches = heads // together
 
     def prepare(i):
@@ -268,11 +297,11 @@
             @pl.when(i == jnp.where(me >= 6, 0, batches - 1))
             def _():
                 relay(None)
-                relay_head(order(0))
+                relay(order(0))
 
     fill_bias(reach)
     loop(prepare, batches)
-    arrivals(None, (1, 3) if tree else range(1, reach + 1))
+    arrivals(None)
     for slot in range(reach):
         fill_bias(slot)
 
@@ -281,45 +310,27 @@
         if tree:
             @pl.when(i + 1 < heads)
             def _():
-                relay_head(order(i + 1))
-
-        for part in range(2):
-            arrivals((h, part), (1, 3) if tree else range(1, reach + 1))
+                relay(order(i + 1))
+
+        arrivals(h)
         attend(h)
 
     loop(step)
 
-    def finish(item):
-        for kind, cond, off in own_sends:
-            @pl.when(cond)
-            def _(kind=kind, off=off):
-                send(item, kind, 0, lax.rem(me + off, n), off).wait_send()
-        if tree:
-            @pl.when(me >= 2)
-            def _():
-                send(item, 3, 2, partner, 1).wait_send()
-
-            @pl.when((me >= 4) & odd)
-            def _():
-                send(item, 4, 4, me - 1, 3).wait_send()
-
-            if item is not None:
-                @pl.when((me >= 6) & (item[0] > 0))
-                def _():
-                    send(item, 5, 4, me - 2, 2).wait_send()
-
-    finish(None)
+    ends = [(kind, cond, win.at[:, :, reach]) for kind, cond, _ in own_sends]
     if tree:
-        @pl.when(straight)
-        def _():
-            for item in (None, (0, 0), (0, 1)):
-                send(item, 6, 0, me + 2, 2).wait_send()
-
-    def finish_head(h):
-        for part in range(2):
-            finish((h, part))
-
-    loop(finish_head)
+        ends += [
+            (3, me >= 2, win.at[:, :, reach]),
+            (4, (me >= 4) & odd, win.at[:, :, reach]),
+            (5, me >= 6, win.at[1:, :, reach]),
+            (6, straight, win.at[0, :, reach]),
+        ]
+    for kind, cond, ref in ends:
+        @pl.when(cond)
+        def _(kind=kind, ref=ref):
+            many(ref, kind=kind).wait_send()
+            if kind != 5:
+                send(None, kind, 0, lax.rem(me + 1, n), 1).wait_send()
 
 
 def local(n, queries, keys, values, doc_ids, counts):
@@ -345,9 +356,9 @@
             pltpu.SMEM(counts.shape, jnp.int32),
             pltpu.SemaphoreType.DMA((2,)),
             pltpu.SemaphoreType.DMA((2,)),
-            pltpu.SemaphoreType.DMA((heads,)),
-            pltpu.SemaphoreType.DMA((heads, 2, 7)),
-            pltpu.SemaphoreType.DMA((heads, 2, reach)),
+            pltpu.SemaphoreType.DMA((heads // math.gcd(heads, 4),)),
+            pltpu.SemaphoreType.DMA((7,)),
+            pltpu.SemaphoreType.DMA((heads, max(reach, 4))),
             pltpu.SemaphoreType.DMA((7,)),
             pltpu.SemaphoreType.DMA((reach,)),
         ],

time: 23.5 us -> 21.5 us (0.915)
  Pallas kernels: 22 us -> 20.1 us
    pallas_call x1, Pallas kernels: 22 us -> 20.1 us  [local(): pl.pallas_call(functools.partial(kernel, n, reach, 512), out_shape=pltpu....]
where the time goes in v3:
time: 21.5 us; the launch traced here: 21.4 us
  Pallas kernels  20.1 us (93%)
  local copies, waits for them, and re-layouts  1.32 us (6%)
    pallas_call x1, Pallas kernels, local(): pl.pallas_call(functools.partial(kernel, n, reach, 512), out_shape=pltpu....  20.1 us
    unnamed x1, local copies, waits for them, and re-layouts  1.32 us

profile of v3, /device:TPU:13, one launch (start us, length us, event | category | flops | bytes accessed | tf_op | source)
XLA Modules:
  0.0 21.4 jit_solution(6620917637752387537)
XLA Ops:
  0.0 20.1 %shard_map.55 = bf16[128,8,8,128]{3,2,1,0:T(8,128)(2,1)S(1)} custom-call(s32[8]{0:T(128)} %counts_hbm.1, bf16[128,8,8,128]{3,2,1,0:T(8,128)(2,1)} %bitcast.4, bf16[128,8,128]{2,1,0:T(8,128)(2,1)} %k_hbm.1, bf16[128,8,128]{2,1,0:T(8,128)(2,1)} %v_hbm.1, s32[1,128]{1,0:T(1,128)} %bitcast.5), custom_call_target="tpu_custom_call" | custom-call | tf_op jit(solution)/shard_map/pallas_call | solution.py:342
  20.1 1.3 %copy.7 = bf16[128,64,128]{2,1,0:T(8,128)(2,1)} copy(bf16[128,64,128]{2,1,0:T(8,128)(2,1)S(1)} %bitcast.3) | data formatting | bytes 4194304

commit v4 on v3

--- a/solution.py
+++ b/solution.py
@@ -30,23 +30,36 @@
     chip_odd = lax.rem(me // 2, 2) == 1
     partner = me + 1 - 2 * lax.rem(me, 2)
     if tree:
+        straight = (me == 2) | (me == 3)
+        last_odd = me == 7
+        send_shift = jnp.where(me >= 2, 1, 0)
+        shift = jnp.where(me >= 6, 1, 0)
+        ahead = jnp.where(last_odd, 1, 0)
         own_sends = [
-            (0, jnp.logical_not(chip_odd), 2),
-            (1, me < 4, 4),
-            (2, even, 1),
+            (0, jnp.logical_not(chip_odd), jnp.where(even, me + 3, me + 2), jnp.where(even, 1, 2)),
+            (1, me < 4, jnp.where(me < 2, me + 4, 7), jnp.where(me == 2, reach + 1, 0)),
+            (2, even, me + 1, reach - 1),
         ]
+        straight_slot = jnp.where(me == 2, 1, 2)
         senders = [
             (odd | (me >= 2), partner),
-            (chip_odd | (me == 4) | (me == 5), me - 2),
-            (me >= 4, me - 4),
-            ((me >= 4) & (me < 6), me + 2),
+            (lax.rem(me, 4) == 3, me - 3),
+            (lax.rem(me, 4) == 3, me - 2),
+            ((me == 4) | (me == 5), me - 4),
+            (last_odd, 2),
+            (last_odd, 3),
+            (me == 5, 7),
+            (me == 5, 2),
+            (me == 5, 3),
         ]
-        targets = [even | (me >= 2), (me < 4) | jnp.logical_not(chip_odd), me < 4, me >= 6]
-        straight = (me == 2) | (me == 3)
-        send_shift = jnp.where(me >= 2, 1, 0)
-        shift = jnp.where(me >= 6, 1, 0)
+        targets = [
+            even, odd & (me >= 3), jnp.logical_not(chip_odd), me < 4, last_odd, straight,
+        ]
     else:
-        own_sends = [(off - 1, me + off < n, off) for off in range(1, reach + 1)]
+        own_sends = [
+            (off - 1, me + off < n, lax.rem(me + off, n), reach - off)
+            for off in range(1, reach + 1)
+        ]
         senders = [(me >= off, me - off) for off in range(1, reach + 1)]
         targets = [me + off < n for off in range(1, reach + 1)]
         send_shift = shift = 0
@@ -79,41 +92,50 @@
 
     loop(lambda h: q_copy(h).start())
 
-    def recv_index(part, off):
+    def recv_index(kind, item):
         if not tree:
-            return off - 1
-        return {1: 3, 2: 0, 3: 3, 4: 1 + part}[off]
-
-    def send(item, kind, from_off, to, to_off):
+            return kind
+        return {1: 1 if item is None else 1 + item[1], 2: 3, 3: 3, 4: 3}.get(kind, 0)
+
+    def send(item, kind, slot, to, to_slot):
         if item is None:
-            src, dst = dwin.at[reach - from_off], dwin.at[reach - to_off]
-            sems = dsend_sem.at[kind], drecv_sem.at[to_off - 1]
+            src, dst = dwin.at[slot], dwin.at[to_slot]
+            sems = dsend_sem.at[kind], drecv_sem.at[recv_index(kind, item)]
         else:
             h, part = item
-            src, dst = win.at[h, part, reach - from_off], win.at[h, part, reach - to_off]
-            sems = send_sem.at[kind], recv_sem.at[h, recv_index(part, to_off)]
+            src, dst = win.at[h, part, slot], win.at[h, part, to_slot]
+            sems = send_sem.at[kind], recv_sem.at[h, recv_index(kind, item)]
         return pltpu.make_async_remote_copy(
             src_ref=src, dst_ref=dst, send_sem=sems[0], recv_sem=sems[1],
             device_id={"seq": to}, device_id_type=MESH,
         )
 
-    def many(ref, kind=0, recv=(0, 0)):
-        return pltpu.make_async_remote_copy(
-            src_ref=ref, dst_ref=ref, send_sem=send_sem.at[kind], recv_sem=recv_sem.at[recv],
+    def blocks_of(h, count):
+        if h is None:
+            return dwin.at[:count]
+        return win.at[h, :, :count] if count > 1 else win.at[h, :, 0]
+
+    def wait_for(h, index, ref):
+        pltpu.make_async_remote_copy(
+            src_ref=ref, dst_ref=ref, send_sem=send_sem.at[0],
+            recv_sem=drecv_sem.at[index] if h is None else recv_sem.at[h, index],
             device_id={"seq": lax.rem(me + 1, n)}, device_id_type=MESH,
-        )
-
-    def wait_block(item, off):
-        send(item, 0, 0, lax.rem(me + 1, n), off).wait_recv()
-
-    def wait_both(h, off):
-        many(win.at[h, :, reach - off], recv=(h, recv_index(0, off))).wait_recv()
+        ).wait_recv()
+
+    def wait_sent(sem, ref):
+        pltpu.make_async_remote_copy(
+            src_ref=ref, dst_ref=ref, send_sem=sem, recv_sem=recv_sem.at[0, 0],
+            device_id={"seq": lax.rem(me + 1, n)}, device_id_type=MESH,
+        ).wait_send()
+
+    def items_of(h):
+        return [None] if h is None else [(h, 0), (h, 1)]
 
     def start_own(item):
-        for kind, cond, off in own_sends:
+        for kind, cond, to, slot in own_sends:
             @pl.when(cond)
-            def _(kind=kind, off=off):
-                send(item, kind, 0, lax.rem(me + off, n), off).start()
+            def _(kind=kind, to=to, slot=slot):
+                send(item, kind, reach, to, slot).start()
 
     doc_copy.wait()
     for part in range(2):
@@ -126,7 +148,7 @@
         @pl.when(straight)
         def _():
             for item in (None, (0, 0), (0, 1)):
-                send(item, 6, 0, me + 2, 2).start()
+                send(item, 6, reach, 5, straight_slot).start()
 
     def start_head(i):
         for part in range(2):
@@ -145,62 +167,58 @@
 
             loop(clear)
 
-    def relay_two(h):
-        if h is None:
-            wait_block(None, 2)
-        else:
-            wait_both(h, 2)
-
-        for item in [None] if h is None else [(h, 0), (h, 1)]:
-            @pl.when(even)
-            def _(item=item):
-                send(item, 3, 2, partner, 3).start()
-
-            @pl.when(odd)
-            def _(item=item):
-                send(item, 3, 2, partner, 1).start()
-
-    def relay_four(item):
-        wait_block(item, 4)
-
-        if item is not None:
-            @pl.when((me >= 6) & (item[0] > 0))
-            def _():
-                send(item, 5, 4, me - 2, 2).start()
-
-        @pl.when(odd)
+    def fetch_y(item):
+        h = None if item is None else item[0]
+
+        def ref(slots):
+            return dwin.at[slots] if item is None else win.at[item[0], item[1], slots]
+
+        @pl.when(last_odd)
         def _():
-            send(item, 4, 4, me - 1, 3).start()
-
-    def relay(h):
-        @pl.when(me >= 4)
+            wait_for(h, recv_index(1, item), ref(slice(0, 2)))
+            if item is not None:
+                @pl.when(h > 0)
+                def _():
+                    send(item, 5, reach + 1, 5, 1).start()
+                    send(item, 5, 0, 5, 2).start()
+
+            send(item, 4, reach + 1, 6, 0).start()
+            send(item, 4, 0, 6, 1).start()
+
+        @pl.when(me == 5)
         def _():
-            for item in [None] if h is None else [(h, 0), (h, 1)]:
-                relay_four(item)
-
-        @pl.when(me >= 2)
+            wait_for(h, recv_index(1, item), ref(0))
+            send(item, 4, 0, 4, 1).start()
+
+    def fetch(h):
+        for item in items_of(h):
+            fetch_y(item)
+
+        @pl.when(odd & (me >= 3))
         def _():
-            relay_two(h)
+            wait_for(h, 0, blocks_of(h, 2))
+            for item in items_of(h):
+                for slot in (1, 2):
+                    send(item, 3, slot, me - 1, slot + 1).start()
 
     def arrivals(h):
-        if h is None:
-            for off in (1, 3) if tree else range(1, reach + 1):
-                @pl.when(me >= off)
-                def _(off=off):
-                    wait_block(None, off)
-        elif tree:
-            @pl.when(me >= 3)
-            def _():
-                many(win.at[h, :, :2], recv=(h, 3)).wait_recv()
-
-            @pl.when((me == 1) | (me == 2))
-            def _():
-                many(win.at[h, :, 0], recv=(h, 3)).wait_recv()
-        else:
+        if not tree:
             for off in range(1, reach + 1):
                 @pl.when(me >= off)
                 def _(off=off):
-                    wait_both(h, off)
+                    wait_for(h, off - 1, blocks_of(h, 1))
+            return
+
+        @pl.when(me == 4)
+        def _():
+            for item in items_of(h):
+                ref = dwin.at[0] if item is None else win.at[item[0], item[1], 0]
+                wait_for(h, recv_index(1, item), ref)
+
+        for cond, count in ((odd, 1), (me == 2, 2), (me == 4, 3), (me == 6, 4)):
+            @pl.when(cond)
+            def _(count=count):
+                wait_for(h, 3, blocks_of(h, count))
 
     lane = lax.broadcasted_iota(jnp.int32, (shard_rows, shard_rows), 1)
     row = lax.broadcasted_iota(jnp.int32, (shard_rows, shard_rows), 0)
@@ -296,8 +314,8 @@
         if tree:
             @pl.when(i == jnp.where(me >= 6, 0, batches - 1))
             def _():
-                relay(None)
-                relay(order(0))
+                fetch(None)
+                fetch(order(0))
 
     fill_bias(reach)
     loop(prepare, batches)
@@ -308,29 +326,31 @@
     def step(i):
         h = order(i)
         if tree:
-            @pl.when(i + 1 < heads)
+            @pl.when((i + ahead > 0) & (i + ahead < heads))
             def _():
-                relay(order(i + 1))
+                fetch(order(i + ahead))
 
         arrivals(h)
         attend(h)
 
     loop(step)
 
-    ends = [(kind, cond, win.at[:, :, reach]) for kind, cond, _ in own_sends]
+    ends = [(kind, cond, win.at[:, :, reach], 1) for kind, cond, _, _ in own_sends]
     if tree:
+        two = win.at[:, :, :2]
         ends += [
-            (3, me >= 2, win.at[:, :, reach]),
-            (4, (me >= 4) & odd, win.at[:, :, reach]),
-            (5, me >= 6, win.at[1:, :, reach]),
-            (6, straight, win.at[0, :, reach]),
+            (3, odd & (me >= 3), two, 2),
+            (4, me == 5, win.at[:, :, reach], 1),
+            (4, last_odd, two, 2),
+            (5, last_odd, win.at[1:, :, :2], 0),
+            (6, straight, win.at[0, :, reach], 1),
         ]
-    for kind, cond, ref in ends:
+    for kind, cond, ref, docs in ends:
         @pl.when(cond)
-        def _(kind=kind, ref=ref):
-            many(ref, kind=kind).wait_send()
-            if kind != 5:
-                send(None, kind, 0, lax.rem(me + 1, n), 1).wait_send()
+        def _(kind=kind, ref=ref, docs=docs):
+            wait_sent(send_sem.at[kind], ref)
+            if docs:
+                wait_sent(dsend_sem.at[kind], dwin.at[:docs])
 
 
 def local(n, queries, keys, values, doc_ids, counts):
@@ -346,9 +366,9 @@
         out_specs=pl.BlockSpec(memory_space=pltpu.VMEM),
         scratch_shapes=[
             pltpu.VMEM((2, shard_rows, heads, width), jnp.bfloat16),
-            pltpu.VMEM((heads, 2, reach + 1, shard_rows, width), jnp.bfloat16),
+            pltpu.VMEM((heads, 2, reach + 2, shard_rows, width), jnp.bfloat16),
             pltpu.VMEM((heads, shard_rows, group, width), jnp.bfloat16),
-            pltpu.VMEM((reach + 1, 1, shard_rows), jnp.int32),
+            pltpu.VMEM((reach + 2, 1, shard_rows), jnp.int32),
             pltpu.VMEM((rows, (reach + 1) * shard_rows), jnp.float32),
             pltpu.VMEM((heads, rows, width), jnp.float32),
             pltpu.VMEM((heads, rows, width), jnp.float32),
@@ -360,7 +380,7 @@
             pltpu.SemaphoreType.DMA((7,)),
             pltpu.SemaphoreType.DMA((heads, max(reach, 4))),
             pltpu.SemaphoreType.DMA((7,)),
-            pltpu.SemaphoreType.DMA((reach,)),
+            pltpu.SemaphoreType.DMA((max(reach, 4),)),
         ],
         compiler_params=pltpu.CompilerParams(
             collective_id=0, has_side_effects=True, vmem_limit_bytes=51 << 20

time: 21.5 us -> 20.3 us (0.944)
  the two profiles are of different devices: /device:TPU:13 before, /device:TPU:12 now
where the time goes in v4:
time: 20.3 us; the launch traced here: 20.1 us
  Pallas kernels  18.8 us (93%)
  local copies, waits for them, and re-layouts  1.32 us (7%)
    pallas_call x1, Pallas kernels, local(): pl.pallas_call(functools.partial(kernel, n, reach, 512), out_shape=pltpu....  18.8 us
    unnamed x1, local copies, waits for them, and re-layouts  1.32 us

profile of v4, /device:TPU:12, one launch (start us, length us, event | category | flops | bytes accessed | tf_op | source)
XLA Modules:
  0.0 20.1 jit_solution(6466930740350691640)
XLA Ops:
  0.0 18.8 %shard_map.55 = bf16[128,8,8,128]{3,2,1,0:T(8,128)(2,1)S(1)} custom-call(s32[8]{0:T(128)} %counts_hbm.1, bf16[128,8,8,128]{3,2,1,0:T(8,128)(2,1)} %bitcast.4, bf16[128,8,128]{2,1,0:T(8,128)(2,1)} %k_hbm.1, bf16[128,8,128]{2,1,0:T(8,128)(2,1)} %v_hbm.1, s32[1,128]{1,0:T(1,128)} %bitcast.5), custom_call_target="tpu_custom_call" | custom-call | tf_op jit(solution)/shard_map/pallas_call | solution.py:362
  18.8 1.3 %copy.7 = bf16[128,64,128]{2,1,0:T(8,128)(2,1)} copy(bf16[128,64,128]{2,1,0:T(8,128)(2,1)S(1)} %bitcast.3) | data formatting | bytes 4194304

commit v5 on v4

--- a/solution.py
+++ b/solution.py
@@ -16,12 +16,13 @@
 def kernel(
     n, reach, tile,
     counts_hbm, q_hbm, k_hbm, v_hbm, docs_hbm, out_ref,
-    raw, win, q_vmem, dwin, bias, top_ref, norm_ref, part_ref, counts_ref, small_sem, raw_sem,
-    q_sem, send_sem, recv_sem, dsend_sem, drecv_sem,
+    raw, win, q_vmem, dwin, bias, weights, top_ref, norm_ref, part_ref, counts_ref, small_sem, raw_sem,
+    q_sem, send_sem, recv_sem, block_sem, dsend_sem, drecv_sem,
 ):
     me = lax.axis_index("seq")
     heads, shard_rows, group, width = q_vmem.shape
     together = math.gcd(heads, 4)
+    own = reach + 1
     rows = shard_rows * group
     tree = n == 8 and reach == 4
 
@@ -36,11 +37,11 @@
         shift = jnp.where(me >= 6, 1, 0)
         ahead = jnp.where(last_odd, 1, 0)
         own_sends = [
-            (0, jnp.logical_not(chip_odd), jnp.where(even, me + 3, me + 2), jnp.where(even, 1, 2)),
-            (1, me < 4, jnp.where(me < 2, me + 4, 7), jnp.where(me == 2, reach + 1, 0)),
-            (2, even, me + 1, reach - 1),
+            (0, jnp.logical_not(chip_odd), jnp.where(even, me + 3, me + 2), jnp.where(even, 2, 3)),
+            (1, me < 4, jnp.where(me < 2, me + 4, 7), jnp.where(me == 2, 0, 1)),
+            (2, even, me + 1, reach),
         ]
-        straight_slot = jnp.where(me == 2, 1, 2)
+        straight_slot = jnp.where(me == 2, 2, 3)
         senders = [
             (odd | (me >= 2), partner),
             (lax.rem(me, 4) == 3, me - 3),
@@ -57,7 +58,7 @@
         ]
     else:
         own_sends = [
-            (off - 1, me + off < n, lax.rem(me + off, n), reach - off)
+            (off - 1, me + off < n, lax.rem(me + off, n), own - off)
             for off in range(1, reach + 1)
         ]
         senders = [(me >= off, me - off) for off in range(1, reach + 1)]
@@ -80,7 +81,7 @@
         pltpu.make_async_copy(ref, raw.at[part], raw_sem.at[part])
         for part, ref in enumerate((k_hbm, v_hbm))
     ]
-    doc_copy = pltpu.make_async_copy(docs_hbm, dwin.at[reach], small_sem.at[0])
+    doc_copy = pltpu.make_async_copy(docs_hbm, dwin.at[own], small_sem.at[0])
     count_copy = pltpu.make_async_copy(counts_hbm, counts_ref, small_sem.at[1])
     doc_copy.start()
     for copy in raw_copies:
@@ -92,28 +93,35 @@
 
     loop(lambda h: q_copy(h).start())
 
+    both = slice(0, 2)
+
+    def where(item, slot):
+        if item is None:
+            return dwin.at[slot]
+        return win.at[item[0], item[1], slot]
+
     def recv_index(kind, item):
         if not tree:
             return kind
-        return {1: 1 if item is None else 1 + item[1], 2: 3, 3: 3, 4: 3}.get(kind, 0)
+        if item is None:
+            return {1: 1, 2: 4, 3: 3, 4: 3}.get(kind, 0)
+        return {1: 2, 3: 4, 4: 4}.get(kind, 0) + item[1]
 
     def send(item, kind, slot, to, to_slot):
-        if item is None:
-            src, dst = dwin.at[slot], dwin.at[to_slot]
-            sems = dsend_sem.at[kind], drecv_sem.at[recv_index(kind, item)]
-        else:
-            h, part = item
-            src, dst = win.at[h, part, slot], win.at[h, part, to_slot]
-            sems = send_sem.at[kind], recv_sem.at[h, recv_index(kind, item)]
+        index = recv_index(kind, item)
         return pltpu.make_async_remote_copy(
-            src_ref=src, dst_ref=dst, send_sem=sems[0], recv_sem=sems[1],
+            src_ref=where(item, slot), dst_ref=where(item, to_slot),
+            send_sem=dsend_sem.at[kind] if item is None else send_sem.at[kind],
+            recv_sem=drecv_sem.at[index] if item is None else recv_sem.at[item[0], index],
             device_id={"seq": to}, device_id_type=MESH,
         )
 
-    def blocks_of(h, count):
-        if h is None:
-            return dwin.at[:count]
-        return win.at[h, :, :count] if count > 1 else win.at[h, :, 0]
+    def send_block():
+        return pltpu.make_async_remote_copy(
+            src_ref=win.at[:, :, own], dst_ref=win.at[:, :, reach],
+            send_sem=send_sem.at[2], recv_sem=block_sem.at[0],
+            device_id={"seq": partner}, device_id_type=MESH,
+        )
 
     def wait_for(h, index, ref):
         pltpu.make_async_remote_copy(
@@ -128,19 +136,20 @@
             device_id={"seq": lax.rem(me + 1, n)}, device_id_type=MESH,
         ).wait_send()
 
-    def items_of(h):
-        return [None] if h is None else [(h, 0), (h, 1)]
-
-    def start_own(item):
+    def start_own(h):
         for kind, cond, to, slot in own_sends:
-            @pl.when(cond)
-            def _(kind=kind, to=to, slot=slot):
-                send(item, kind, reach, to, slot).start()
+            if h is not None and tree and kind == 2:
+                continue
+            parts = [0, 1] if tree else [both]
+            for item in [None] if h is None else [(h, part) for part in parts]:
+                @pl.when(cond)
+                def _(item=item, kind=kind, to=to, slot=slot):
+                    send(item, kind, own, to, slot).start()
 
     doc_copy.wait()
     for part in range(2):
         raw_copies[part].wait()
-        win[:, part, reach] = jnp.swapaxes(raw[part], 0, 1)
+        win[:, part, own] = jnp.swapaxes(raw[part], 0, 1)
     pl.semaphore_wait(barrier, sum(jnp.where(cond, 1, 0) for cond in targets))
 
     start_own(None)
@@ -148,86 +157,92 @@
         @pl.when(straight)
         def _():
             for item in (None, (0, 0), (0, 1)):
-                send(item, 6, reach, 5, straight_slot).start()
+                send(item, 6, own, 5, straight_slot).start()
 
     def start_head(i):
-        for part in range(2):
-            start_own((lax.rem(i + send_shift, heads), part))
+        start_own(lax.rem(i + send_shift, heads))
 
     loop(start_head)
+    if tree:
+        @pl.when(even)
+        def _():
+            send_block().start()
+
     count_copy.wait()
 
     for off in range(1, reach + 1):
         @pl.when(me < off)
         def _(off=off):
-            dwin[reach - off] = jnp.full(dwin.shape[1:], -1, jnp.int32)
+            dwin[own - off] = jnp.full(dwin.shape[1:], -1, jnp.int32)
 
             def clear(h):
-                win[h, :, reach - off] = jnp.zeros((2, shard_rows, width), win.dtype)
+                win[h, :, own - off] = jnp.zeros((2, shard_rows, width), win.dtype)
 
             loop(clear)
 
     def fetch_y(item):
         h = None if item is None else item[0]
-
-        def ref(slots):
-            return dwin.at[slots] if item is None else win.at[item[0], item[1], slots]
+        index = recv_index(1, item)
+        two = slice(0, 2)
 
         @pl.when(last_odd)
         def _():
-            wait_for(h, recv_index(1, item), ref(slice(0, 2)))
+            wait_for(h, index, where(item, two))
             if item is not None:
                 @pl.when(h > 0)
                 def _():
-                    send(item, 5, reach + 1, 5, 1).start()
-                    send(item, 5, 0, 5, 2).start()
-
-            send(item, 4, reach + 1, 6, 0).start()
-            send(item, 4, 0, 6, 1).start()
+                    send(item, 5, two, 5, slice(2, 4)).start()
+
+            send(item, 4, two, 6, slice(1, 3)).start()
 
         @pl.when(me == 5)
         def _():
-            wait_for(h, recv_index(1, item), ref(0))
-            send(item, 4, 0, 4, 1).start()
-
-    def fetch(h):
-        for item in items_of(h):
-            fetch_y(item)
+            wait_for(h, index, where(item, 1))
+            send(item, 4, 1, 4, 2).start()
+
+    def fetch(item):
+        fetch_y(item)
 
         @pl.when(odd & (me >= 3))
         def _():
-            wait_for(h, 0, blocks_of(h, 2))
-            for item in items_of(h):
-                for slot in (1, 2):
-                    send(item, 3, slot, me - 1, slot + 1).start()
-
-    def arrivals(h):
+            h = None if item is None else item[0]
+            wait_for(h, recv_index(0, item), where(item, slice(0, 2)))
+            send(item, 3, slice(2, 4), me - 1, slice(3, 5)).start()
+
+    def arrivals(item):
+        h = None if item is None else item[0]
         if not tree:
             for off in range(1, reach + 1):
                 @pl.when(me >= off)
                 def _(off=off):
-                    wait_for(h, off - 1, blocks_of(h, 1))
+                    wait_for(h, off - 1, where(item, slice(0, 1)))
             return
 
         @pl.when(me == 4)
         def _():
-            for item in items_of(h):
-                ref = dwin.at[0] if item is None else win.at[item[0], item[1], 0]
-                wait_for(h, recv_index(1, item), ref)
-
-        for cond, count in ((odd, 1), (me == 2, 2), (me == 4, 3), (me == 6, 4)):
+            wait_for(h, recv_index(1, item), where(item, 1))
+
+        for cond, count in ((me == 2, 2), (me == 4, 3), (me == 6, 4)):
             @pl.when(cond)
             def _(count=count):
-                wait_for(h, 3, blocks_of(h, count))
+                wait_for(h, recv_index(3, item), where(item, slice(0, count)))
+
+    def arrivals_first():
+        arrivals(None)
+        if tree:
+            @pl.when(odd)
+            def _():
+                wait_for(None, 4, dwin.at[:1])
+                send_block().wait_recv()
 
     lane = lax.broadcasted_iota(jnp.int32, (shard_rows, shard_rows), 1)
     row = lax.broadcasted_iota(jnp.int32, (shard_rows, shard_rows), 0)
-    doc_col = jnp.transpose(jnp.broadcast_to(dwin[reach], (shard_rows, shard_rows)))
+    doc_col = jnp.transpose(jnp.broadcast_to(dwin[own], (shard_rows, shard_rows)))
 
     def fill_bias(slot):
         off = reach - slot
         count = counts_ref[lax.max(me - off, 0)]
-        docs = dwin[slot]
+        docs = dwin[slot + 1]
         allowed = (docs == doc_col) & (lane < count)
         if off == 0:
             allowed = allowed & (lane <= row)
@@ -254,7 +269,7 @@
     def own_scores(h):
         q = q_vmem[h].reshape(rows, width)
         return lax.dot_general(
-            q, win[h, 0, reach], (((1,), (1,)), ((), ())), preferred_element_type=jnp.float32
+            q, win[h, 0, own], (((1,), (1,)), ((), ())), preferred_element_type=jnp.float32
         )
 
     def own_weights(h, s):
@@ -265,7 +280,7 @@
 
     def own_mix(h, p):
         ones = jnp.ones((shard_rows, width), jnp.bfloat16)
-        o = mix(p, jnp.concatenate([win[h, 1, reach], ones], axis=1))
+        o = mix(p, jnp.concatenate([win[h, 1, own], ones], axis=1))
         part_ref[h] = o[:, :width]
         norm_ref[h] = o[:, width:]
 
@@ -282,9 +297,8 @@
             if k >= 2:
                 own_mix(hs[k - 2], p.pop(k - 2))
 
-    def attend(h):
-        keys = win[h, 0, :reach].reshape(remote, width)
-        values = win[h, 1, :reach].reshape(remote, width)
+    def attend_keys(h):
+        keys = win[h, 0, 1:own].reshape(remote, width)
         s_next = scores(h, 0, keys)
         for start in range(0, rows, tile):
             at = slice(start, start + tile)
@@ -295,11 +309,18 @@
             own_top = top_ref[h, at]
             top = jnp.maximum(jnp.max(x, axis=-1, keepdims=True), own_top)
             p = jnp.exp2(x - jnp.concatenate([top] * reach, axis=1))
-            own = jnp.exp2(own_top - top)
-            norm = jnp.sum(p, axis=-1, keepdims=True) + own * norm_ref[h, at]
-            o = mix(p, values) + own * part_ref[h, at]
+            scale = jnp.exp2(own_top - top)
+            weights[at] = p.astype(jnp.bfloat16)
+            top_ref[h, at] = scale
+            norm_ref[h, at] = jnp.sum(p, axis=-1, keepdims=True) + scale * norm_ref[h, at]
+
+    def attend_values(h):
+        values = win[h, 1, 1:own].reshape(remote, width)
+        for start in range(0, rows, tile):
+            at = slice(start, start + tile)
+            o = mix(weights[at], values) + top_ref[h, at] * part_ref[h, at]
             r = lax.broadcasted_iota(jnp.int32, (tile, width), 0) + start
-            o = jnp.where(r < own_count * group, o / norm, 0.0).astype(jnp.bfloat16)
+            o = jnp.where(r < own_count * group, o / norm_ref[h, at], 0.0).astype(jnp.bfloat16)
             out_ref[start // group : (start + tile) // group, h] = o.reshape(
                 tile // group, group, width
             )
@@ -307,43 +328,40 @@
     def order(i):
         return lax.rem(i + shift, heads)
 
-    batches = heads // together
-
-    def prepare(i):
-        attend_own(i)
-        if tree:
-            @pl.when(i == jnp.where(me >= 6, 0, batches - 1))
-            def _():
-                fetch(None)
-                fetch(order(0))
-
     fill_bias(reach)
-    loop(prepare, batches)
-    arrivals(None)
+    loop(attend_own, heads // together)
+    if tree:
+        for item in (None, (order(0), 0), (order(0), 1)):
+            fetch(item)
+    arrivals_first()
     for slot in range(reach):
         fill_bias(slot)
 
     def step(i):
         h = order(i)
-        if tree:
-            @pl.when((i + ahead > 0) & (i + ahead < heads))
-            def _():
-                fetch(order(i + ahead))
-
-        arrivals(h)
-        attend(h)
+        for part, attend in enumerate((attend_keys, attend_values)):
+            if tree:
+                @pl.when((i + ahead > 0) & (i + ahead < heads))
+                def _(part=part):
+                    fetch((order(i + ahead), part))
+
+            if tree:
+                arrivals((h, part))
+            elif part == 0:
+                arrivals((h, both))
+            attend(h)
 
     loop(step)
 
-    ends = [(kind, cond, win.at[:, :, reach], 1) for kind, cond, _, _ in own_sends]
+    one, two = win.at[:, :, own], win.at[:, :, :2]
+    ends = [(kind, cond, one, 1) for kind, cond, _, _ in own_sends]
     if tree:
-        two = win.at[:, :, :2]
         ends += [
             (3, odd & (me >= 3), two, 2),
-            (4, me == 5, win.at[:, :, reach], 1),
+            (4, me == 5, one, 1),
             (4, last_odd, two, 2),
             (5, last_odd, win.at[1:, :, :2], 0),
-            (6, straight, win.at[0, :, reach], 1),
+            (6, straight, win.at[0, :, own], 1),
         ]
     for kind, cond, ref, docs in ends:
         @pl.when(cond)
@@ -370,6 +388,7 @@
             pltpu.VMEM((heads, shard_rows, group, width), jnp.bfloat16),
             pltpu.VMEM((reach + 2, 1, shard_rows), jnp.int32),
             pltpu.VMEM((rows, (reach + 1) * shard_rows), jnp.float32),
+            pltpu.VMEM((rows, reach * shard_rows), jnp.bfloat16),
             pltpu.VMEM((heads, rows, width), jnp.float32),
             pltpu.VMEM((heads, rows, width), jnp.float32),
             pltpu.VMEM((heads, rows, width), jnp.float32),
@@ -378,9 +397,10 @@
             pltpu.SemaphoreType.DMA((2,)),
             pltpu.SemaphoreType.DMA((heads // math.gcd(heads, 4),)),
             pltpu.SemaphoreType.DMA((7,)),
-            pltpu.SemaphoreType.DMA((heads, max(reach, 4))),
+            pltpu.SemaphoreType.DMA((heads, max(reach, 6))),
+            pltpu.SemaphoreType.DMA((1,)),
             pltpu.SemaphoreType.DMA((7,)),
-            pltpu.SemaphoreType.DMA((max(reach, 4),)),
+            pltpu.SemaphoreType.DMA((max(reach, 5),)),
         ],
         compiler_params=pltpu.CompilerParams(
             collective_id=0, has_side_effects=True, vmem_limit_bytes=51 << 20

time: 20.3 us -> 19.4 us (0.956)
  the two profiles are of different devices: /device:TPU:12 before, /device:TPU:13 now
where the time goes in v5:
time: 19.4 us; the launch traced here: 19.2 us
  Pallas kernels  17.8 us (92%)
  local copies, waits for them, and re-layouts  1.32 us (7%)
    pallas_call x1, Pallas kernels, local(): pl.pallas_call(functools.partial(kernel, n, reach, 512), out_shape=pltpu....  17.8 us
    unnamed x1, local copies, waits for them, and re-layouts  1.32 us

profile of v5, /device:TPU:13, one launch (start us, length us, event | category | flops | bytes accessed | tf_op | source)
XLA Modules:
  0.0 19.2 jit_solution(9509061905867978137)
XLA Ops:
  0.0 17.8 %shard_map.55 = bf16[128,8,8,128]{3,2,1,0:T(8,128)(2,1)S(1)} custom-call(s32[8]{0:T(128)} %counts_hbm.1, bf16[128,8,8,128]{3,2,1,0:T(8,128)(2,1)} %bitcast.4, bf16[128,8,128]{2,1,0:T(8,128)(2,1)} %k_hbm.1, bf16[128,8,128]{2,1,0:T(8,128)(2,1)} %v_hbm.1, s32[1,128]{1,0:T(1,128)} %bitcast.5), custom_call_target="tpu_custom_call" | custom-call | tf_op jit(solution)/shard_map/pallas_call | solution.py:380
  17.8 1.3 %copy.7 = bf16[128,64,128]{2,1,0:T(8,128)(2,1)} copy(bf16[128,64,128]{2,1,0:T(8,128)(2,1)S(1)} %bitcast.3) | data formatting | bytes 4194304

commit v6 on v5

--- a/solution.py
+++ b/solution.py
@@ -78,7 +78,7 @@
         lax.fori_loop(0, heads if count is None else count, lambda i, c: (body(i), c)[1], 0)
 
     raw_copies = [
-        pltpu.make_async_copy(ref, raw.at[part], raw_sem.at[part])
+        pltpu.make_async_copy(ref, raw.at[part], raw_sem.at[0])
         for part, ref in enumerate((k_hbm, v_hbm))
     ]
     doc_copy = pltpu.make_async_copy(docs_hbm, dwin.at[own], small_sem.at[0])
@@ -89,7 +89,7 @@
     count_copy.start()
 
     def q_copy(h):
-        return pltpu.make_async_copy(q_hbm.at[:, h], q_vmem.at[h], q_sem.at[h // together])
+        return pltpu.make_async_copy(q_hbm.at[:, h], q_vmem.at[h], q_sem.at[0])
 
     loop(lambda h: q_copy(h).start())
 
@@ -104,14 +104,14 @@
         if not tree:
             return kind
         if item is None:
-            return {1: 1, 2: 4, 3: 3, 4: 3}.get(kind, 0)
-        return {1: 2, 3: 4, 4: 4}.get(kind, 0) + item[1]
+            return {1: 1, 2: 2}.get(kind, 0)
+        return (2 if kind == 1 else 0) + item[1]
 
     def send(item, kind, slot, to, to_slot):
         index = recv_index(kind, item)
         return pltpu.make_async_remote_copy(
             src_ref=where(item, slot), dst_ref=where(item, to_slot),
-            send_sem=dsend_sem.at[kind] if item is None else send_sem.at[kind],
+            send_sem=dsend_sem.at[0] if item is None else send_sem.at[kind],
             recv_sem=drecv_sem.at[index] if item is None else recv_sem.at[item[0], index],
             device_id={"seq": to}, device_id_type=MESH,
         )
@@ -147,8 +147,8 @@
                     send(item, kind, own, to, slot).start()
 
     doc_copy.wait()
+    pltpu.make_async_copy(raw, raw, raw_sem.at[0]).wait()
     for part in range(2):
-        raw_copies[part].wait()
         win[:, part, own] = jnp.swapaxes(raw[part], 0, 1)
     pl.semaphore_wait(barrier, sum(jnp.where(cond, 1, 0) for cond in targets))
 
@@ -232,7 +232,7 @@
         if tree:
             @pl.when(odd)
             def _():
-                wait_for(None, 4, dwin.at[:1])
+                wait_for(None, 2, dwin.at[:1])
                 send_block().wait_recv()
 
     lane = lax.broadcasted_iota(jnp.int32, (shard_rows, shard_rows), 1)
@@ -286,8 +286,6 @@
 
     def attend_own(i):
         hs = [i * together + u for u in range(together)]
-        all_q = q_vmem.at[pl.ds(i * together, together)]
-        pltpu.make_async_copy(all_q, all_q, q_sem.at[i]).wait()
         s, p = {}, {}
         for k in range(together + 2):
             if k < together:
@@ -329,6 +327,7 @@
         return lax.rem(i + shift, heads)
 
     fill_bias(reach)
+    pltpu.make_async_copy(q_vmem, q_vmem, q_sem.at[0]).wait()
     loop(attend_own, heads // together)
     if tree:
         for item in (None, (order(0), 0), (order(0), 1)):
@@ -363,12 +362,16 @@
             (5, last_odd, win.at[1:, :, :2], 0),
             (6, straight, win.at[0, :, own], 1),
         ]
-    for kind, cond, ref, docs in ends:
+    for kind, cond, ref, _ in ends:
         @pl.when(cond)
-        def _(kind=kind, ref=ref, docs=docs):
+        def _(kind=kind, ref=ref):
             wait_sent(send_sem.at[kind], ref)
-            if docs:
-                wait_sent(dsend_sem.at[kind], dwin.at[:docs])
+
+    sent = sum(jnp.where(cond, docs, 0) for _, cond, _, docs in ends)
+    for count in range(1, max(reach, 4) + 1):
+        @pl.when(sent == count)
+        def _(count=count):
+            wait_sent(dsend_sem.at[0], dwin.at[:count])
 
 
 def local(n, queries, keys, values, doc_ids, counts):
@@ -394,13 +397,13 @@
             pltpu.VMEM((heads, rows, width), jnp.float32),
             pltpu.SMEM(counts.shape, jnp.int32),
             pltpu.SemaphoreType.DMA((2,)),
-            pltpu.SemaphoreType.DMA((2,)),
-            pltpu.SemaphoreType.DMA((heads // math.gcd(heads, 4),)),
-            pltpu.SemaphoreType.DMA((7,)),
-            pltpu.SemaphoreType.DMA((heads, max(reach, 6))),
+            pltpu.SemaphoreType.DMA((1,)),
             pltpu.SemaphoreType.DMA((1,)),
             pltpu.SemaphoreType.DMA((7,)),
-            pltpu.SemaphoreType.DMA((max(reach, 5),)),
+            pltpu.SemaphoreType.DMA((heads, max(reach, 4))),
+            pltpu.SemaphoreType.DMA((1,)),
+            pltpu.SemaphoreType.DMA((1,)),
+            pltpu.SemaphoreType.DMA((max(reach, 3),)),
         ],
         compiler_params=pltpu.CompilerParams(
             collective_id=0, has_side_effects=True, vmem_limit_bytes=51 << 20

time: 19.4 us -> 19.3 us (level)
  no operation moved by 1% of the time
where the time goes in v6:
time: 19.3 us; the launch traced here: 19 us
  Pallas kernels  17.7 us (92%)
  local copies, waits for them, and re-layouts  1.32 us (7%)
    pallas_call x1, Pallas kernels, local(): pl.pallas_call(functools.partial(kernel, n, reach, 512), out_shape=pltpu....  17.7 us
    unnamed x1, local copies, waits for them, and re-layouts  1.32 us

profile of v6, /device:TPU:13, one launch (start us, length us, event | category | flops | bytes accessed | tf_op | source)
XLA Modules:
  0.0 19.0 jit_solution(2860119476309264290)
XLA Ops:
  0.0 17.7 %shard_map.55 = bf16[128,8,8,128]{3,2,1,0:T(8,128)(2,1)S(1)} custom-call(s32[8]{0:T(128)} %counts_hbm.1, bf16[128,8,8,128]{3,2,1,0:T(8,128)(2,1)} %bitcast.4, bf16[128,8,128]{2,1,0:T(8,128)(2,1)} %k_hbm.1, bf16[128,8,128]{2,1,0:T(8,128)(2,1)} %v_hbm.1, s32[1,128]{1,0:T(1,128)} %bitcast.5), custom_call_target="tpu_custom_call" | custom-call | tf_op jit(solution)/shard_map/pallas_call | solution.py:383
  17.7 1.3 %copy.7 = bf16[128,64,128]{2,1,0:T(8,128)(2,1)} copy(bf16[128,64,128]{2,1,0:T(8,128)(2,1)S(1)} %bitcast.3) | data formatting | bytes 4194304

commit v7 on v6

--- a/solution.py
+++ b/solution.py
@@ -13,10 +13,53 @@
 NEG = -1e30
 
 
+def mix(p, values):
+    return lax.dot_general(
+        p.astype(jnp.bfloat16), values, (((1,), (0,)), ((), ())),
+        preferred_element_type=jnp.float32,
+    )
+
+
+def mixed(weights, values, scale, part, norm):
+    return ((mix(weights, values) + scale * part) / norm).astype(jnp.bfloat16)
+
+
+def first_head(n, tree):
+    return jnp.where(lax.axis_index("seq") >= 6, 1, 0) if tree else 0
+
+
+def finish_kernel(
+    n, tree, tile,
+    mixed_ref, weights, top_ref, norm_ref, part_ref, values, out_hbm, last, sem,
+):
+    rows, remote = weights.shape
+    shard_rows, heads, group, width = mixed_ref.shape
+    first = first_head(n, tree)
+
+    def copy(i, c):
+        h = lax.rem(i + first, heads)
+        pltpu.make_async_copy(mixed_ref.at[:, h], out_hbm.at[:, h], sem.at[0]).start()
+        return c
+
+    lax.fori_loop(0, heads - 1, copy, 0)
+    h = lax.rem(heads - 1 + first, heads)
+    for start in range(0, rows, tile):
+        at = slice(start, start + tile)
+        places = slice(start // group, (start + tile) // group)
+        last[places] = mixed(
+            weights[at], values[...], top_ref[h, at], part_ref[h, at], norm_ref[h, at],
+        ).reshape(tile // group, group, width)
+        pltpu.make_async_copy(last.at[places], out_hbm.at[places, h], sem.at[1]).start()
+    rest = mixed_ref.at[:, 1:]
+    pltpu.make_async_copy(rest, rest, sem.at[0]).wait()
+    pltpu.make_async_copy(last, last, sem.at[1]).wait()
+
+
 def kernel(
     n, reach, tile,
-    counts_hbm, q_hbm, k_hbm, v_hbm, docs_hbm, out_ref,
-    raw, win, q_vmem, dwin, bias, weights, top_ref, norm_ref, part_ref, counts_ref, small_sem, raw_sem,
+    counts_hbm, q_hbm, k_hbm, v_hbm, docs_hbm,
+    out_ref, weights, top_ref, norm_ref, part_ref, last_values,
+    raw, win, q_vmem, dwin, bias, counts_ref, small_sem, raw_sem,
     q_sem, send_sem, recv_sem, block_sem, dsend_sem, drecv_sem,
 ):
     me = lax.axis_index("seq")
@@ -34,7 +77,6 @@
         straight = (me == 2) | (me == 3)
         last_odd = me == 7
         send_shift = jnp.where(me >= 2, 1, 0)
-        shift = jnp.where(me >= 6, 1, 0)
         ahead = jnp.where(last_odd, 1, 0)
         own_sends = [
             (0, jnp.logical_not(chip_odd), jnp.where(even, me + 3, me + 2), jnp.where(even, 2, 3)),
@@ -63,7 +105,7 @@
         ]
         senders = [(me >= off, me - off) for off in range(1, reach + 1)]
         targets = [me + off < n for off in range(1, reach + 1)]
-        send_shift = shift = 0
+        send_shift = 0
 
     barrier = pltpu.get_barrier_semaphore()
     for cond, device in senders:
@@ -258,12 +300,6 @@
         q = q_vmem[h, start // group : (start + tile) // group].reshape(tile, width)
         return lax.dot_general(
             q, keys, (((1,), (1,)), ((), ())), preferred_element_type=jnp.float32
-        )
-
-    def mix(p, values):
-        return lax.dot_general(
-            p.astype(jnp.bfloat16), values, (((1,), (0,)), ((), ())),
-            preferred_element_type=jnp.float32,
         )
 
     def own_scores(h):
@@ -310,18 +346,19 @@
             scale = jnp.exp2(own_top - top)
             weights[at] = p.astype(jnp.bfloat16)
             top_ref[h, at] = scale
-            norm_ref[h, at] = jnp.sum(p, axis=-1, keepdims=True) + scale * norm_ref[h, at]
+            norm = jnp.sum(p, axis=-1, keepdims=True) + scale * norm_ref[h, at]
+            r = lax.broadcasted_iota(jnp.int32, (tile, width), 0) + start
+            norm_ref[h, at] = jnp.where(r < own_count * group, norm, jnp.inf)
 
     def attend_values(h):
-        values = win[h, 1, 1:own].reshape(remote, width)
         for start in range(0, rows, tile):
             at = slice(start, start + tile)
-            o = mix(weights[at], values) + top_ref[h, at] * part_ref[h, at]
-            r = lax.broadcasted_iota(jnp.int32, (tile, width), 0) + start
-            o = jnp.where(r < own_count * group, o / norm_ref[h, at], 0.0).astype(jnp.bfloat16)
-            out_ref[start // group : (start + tile) // group, h] = o.reshape(
-                tile // group, group, width
-            )
+            out_ref[start // group : (start + tile) // group, h] = mixed(
+                weights[at], win[h, 1, 1:own].reshape(remote, width),
+                top_ref[h, at], part_ref[h, at], norm_ref[h, at],
+            ).reshape(tile // group, group, width)
+
+    shift = first_head(n, tree)
 
     def order(i):
         return lax.rem(i + shift, heads)
@@ -338,19 +375,33 @@
 
     def step(i):
         h = order(i)
-        for part, attend in enumerate((attend_keys, attend_values)):
+        for part in range(2):
             if tree:
-                @pl.when((i + ahead > 0) & (i + ahead < heads))
+                ready = (i + ahead > 0) & (i + ahead < heads)
+                early = ready & (i == heads - 1)
+
+                @pl.when(ready if part == 0 else ready & jnp.logical_not(early))
                 def _(part=part):
                     fetch((order(i + ahead), part))
+
+                if part == 0:
+                    @pl.when(early)
+                    def _():
+                        fetch((h, 1))
 
             if tree:
                 arrivals((h, part))
             elif part == 0:
                 arrivals((h, both))
-            attend(h)
+            if part == 0:
+                attend_keys(h)
+            else:
+                @pl.when(i < heads - 1)
+                def _():
+                    attend_values(h)
 
     loop(step)
+    last_values[...] = win[order(heads - 1), 1, 1:own].reshape(remote, width)
 
     one, two = win.at[:, :, own], win.at[:, :, :2]
     ends = [(kind, cond, one, 1) for kind, cond, _, _ in own_sends]
@@ -380,21 +431,28 @@
     group = q_heads // heads
     reach = min((DOC_MOST + shard_rows - 1) // shard_rows, n - 1)
     rows = shard_rows * group
-    out = pl.pallas_call(
+    tree = n == 8 and reach == 4
+    shape = (shard_rows, heads, group, width)
+    remote = reach * shard_rows
+    saved = pltpu.VMEM((heads, rows, width), jnp.float32)
+    outs = pl.pallas_call(
         functools.partial(kernel, n, reach, 512),
-        out_shape=pltpu.VMEM((shard_rows, heads, group, width), jnp.bfloat16),
+        out_shape=(
+            pltpu.VMEM(shape, jnp.bfloat16),
+            pltpu.VMEM((rows, remote), jnp.bfloat16),
+            saved,
+            saved,
+            saved,
+            pltpu.VMEM((remote, width), jnp.bfloat16),
+        ),
         in_specs=[pl.BlockSpec(memory_space=pltpu.HBM)] * 5,
-        out_specs=pl.BlockSpec(memory_space=pltpu.VMEM),
+        out_specs=[pl.BlockSpec(memory_space=pltpu.VMEM)] * 6,
         scratch_shapes=[
             pltpu.VMEM((2, shard_rows, heads, width), jnp.bfloat16),
             pltpu.VMEM((heads, 2, reach + 2, shard_rows, width), jnp.bfloat16),
             pltpu.VMEM((heads, shard_rows, group, width), jnp.bfloat16),
             pltpu.VMEM((reach + 2, 1, shard_rows), jnp.int32),
             pltpu.VMEM((rows, (reach + 1) * shard_rows), jnp.float32),
-            pltpu.VMEM((rows, reach * shard_rows), jnp.bfloat16),
-            pltpu.VMEM((heads, rows, width), jnp.float32),
-            pltpu.VMEM((heads, rows, width), jnp.float32),
-            pltpu.VMEM((heads, rows, width), jnp.float32),
             pltpu.SMEM(counts.shape, jnp.int32),
             pltpu.SemaphoreType.DMA((2,)),
             pltpu.SemaphoreType.DMA((1,)),
@@ -406,7 +464,7 @@
             pltpu.SemaphoreType.DMA((max(reach, 3),)),
         ],
         compiler_params=pltpu.CompilerParams(
-            collective_id=0, has_side_effects=True, vmem_limit_bytes=51 << 20
+            collective_id=0, has_side_effects=True, vmem_limit_bytes=30 << 20
         ),
     )(
         *(
@@ -420,6 +478,17 @@
             )
         )
     )
+    out = pl.pallas_call(
+        functools.partial(finish_kernel, n, tree, 512),
+        out_shape=jax.ShapeDtypeStruct(shape, jnp.bfloat16),
+        in_specs=[pl.BlockSpec(memory_space=pltpu.VMEM)] * 6,
+        out_specs=pl.BlockSpec(memory_space=pltpu.HBM),
+        scratch_shapes=[
+            pltpu.VMEM((shard_rows, group, width), jnp.bfloat16),
+            pltpu.SemaphoreType.DMA((2,)),
+        ],
+        compiler_params=pltpu.CompilerParams(vmem_limit_bytes=16 << 20),
+    )(*(pltpu.with_memory_space_constraint(x, pltpu.VMEM) for x in outs))
     return out.reshape(shard_rows, q_heads, width)
 
 

time: 19.3 us -> 19 us (0.984)
  local copies, waits for them, and re-layouts: 1.32 us -> 0 us
  Pallas kernels: 17.7 us -> 18.8 us
    unnamed x1 -> x0, local copies, waits for them, and re-layouts: 1.32 us -> none
    pallas_call x1 -> x2, Pallas kernels: 17.7 us -> 18.8 us  [the longest x1 17.4 us: local(): pl.pallas_call(functools.partial(kernel, n, reach, 512), out_shape=(pltpu...]
where the time goes in v7:
time: 19 us; the launch traced here: 18.8 us
  Pallas kernels  18.8 us (99%)
    pallas_call x1, Pallas kernels, local(): pl.pallas_call(functools.partial(kernel, n, reach, 512), out_shape=(pltpu...  17.4 us
    pallas_call x1, Pallas kernels, local(): pl.pallas_call(functools.partial(finish_kernel, n, tree, 512), out_shape=...  1.33 us

profile of v7, /device:TPU:13, one launch (start us, length us, event | category | flops | bytes accessed | tf_op | source)
XLA Modules:
  0.0 18.8 jit_solution(416490507713758676)
XLA Ops:
  0.0 17.4 %shard_map.55 = (bf16[128,8,8,128]{3,2,1,0:T(8,128)(2,1)S(1)}, bf16[1024,512]{1,0:T(8,128)(2,1)S(1)}, f32[8,1024,128]{2,1,0:T(8,128)S(1)}, f32[8,1024,128]{2,1,0...) custom-call(s32[8]{0:T(128)} %counts_hbm.1, bf16[128,8,8,128]{3,2,1,0:T(8,128)(2,1)} %bitcast.3, ...), custom_call_target="tpu_custom_call" | custom-call | tf_op jit(solution)/shard_map/pallas_call | solution.py:438
  17.4 1.3 %shard_map.56 = bf16[128,8,8,128]{3,2,1,0:T(8,128)(2,1)} custom-call(bf16[128,8,8,128]{3,2,1,0:T(8,128)(2,1)S(1)} %get-tuple-element.11.mixed_ref, bf16[1024,512]{1,0:T(8,128)(2,1)S(1)} %get-tuple-element.12.weights, f32[8,1024,128]{2,1,0:T(8,128)S(1)} %get-tuple-element.13.top_ref, f32[8,1024,128]{2,1,0:T(8,128)S(1)} %get-tuple-element.14.norm_ref, ...), custom_call_target="tpu_custom_call" | custom-call | tf_op jit(solution)/shard_map/pallas_call | solution.py:481

commit v8 on v7

--- a/solution.py
+++ b/solution.py
@@ -153,7 +153,7 @@
         index = recv_index(kind, item)
         return pltpu.make_async_remote_copy(
             src_ref=where(item, slot), dst_ref=where(item, to_slot),
-            send_sem=dsend_sem.at[0] if item is None else send_sem.at[kind],
+            send_sem=dsend_sem.at[0] if item is None else send_sem.at[0],
             recv_sem=drecv_sem.at[index] if item is None else recv_sem.at[item[0], index],
             device_id={"seq": to}, device_id_type=MESH,
         )
@@ -161,7 +161,7 @@
     def send_block():
         return pltpu.make_async_remote_copy(
             src_ref=win.at[:, :, own], dst_ref=win.at[:, :, reach],
-            send_sem=send_sem.at[2], recv_sem=block_sem.at[0],
+            send_sem=send_sem.at[0], recv_sem=block_sem.at[0],
             device_id={"seq": partner}, device_id_type=MESH,
         )
 
@@ -403,22 +403,25 @@
     loop(step)
     last_values[...] = win[order(heads - 1), 1, 1:own].reshape(remote, width)
 
-    one, two = win.at[:, :, own], win.at[:, :, :2]
-    ends = [(kind, cond, one, 1) for kind, cond, _, _ in own_sends]
+    one, two = 2 * heads, 4 * heads
+    ends = [(cond, one, 1) for _, cond, _, _ in own_sends]
+    totals = {one * count for count in range(1, reach + 1)}
     if tree:
         ends += [
-            (3, odd & (me >= 3), two, 2),
-            (4, me == 5, one, 1),
-            (4, last_odd, two, 2),
-            (5, last_odd, win.at[1:, :, :2], 0),
-            (6, straight, win.at[0, :, own], 1),
+            (odd & (me >= 3), two, 2),
+            (me == 5, one, 1),
+            (last_odd, two, 2),
+            (last_odd, two - 4, 0),
+            (straight, 2, 1),
         ]
-    for kind, cond, ref, _ in ends:
-        @pl.when(cond)
-        def _(kind=kind, ref=ref):
-            wait_sent(send_sem.at[kind], ref)
-
-    sent = sum(jnp.where(cond, docs, 0) for _, cond, _, docs in ends)
+        totals |= {2 * one + 2, two + one + 2, 3 * two - 4}
+    total = sum(jnp.where(cond, blocks, 0) for cond, blocks, _ in ends)
+    for count in sorted(totals):
+        @pl.when(total == count)
+        def _(count=count):
+            wait_sent(send_sem.at[0], part_ref.at[:, : count * shard_rows // (2 * heads)])
+
+    sent = sum(jnp.where(cond, docs, 0) for cond, _, docs in ends)
     for count in range(1, max(reach, 4) + 1):
         @pl.when(sent == count)
         def _(count=count):
@@ -457,7 +460,7 @@
             pltpu.SemaphoreType.DMA((2,)),
             pltpu.SemaphoreType.DMA((1,)),
             pltpu.SemaphoreType.DMA((1,)),
-            pltpu.SemaphoreType.DMA((7,)),
+            pltpu.SemaphoreType.DMA((1,)),
             pltpu.SemaphoreType.DMA((heads, max(reach, 4))),
             pltpu.SemaphoreType.DMA((1,)),
             pltpu.SemaphoreType.DMA((1,)),

time: 19 us -> 18.9 us (level)
  no operation moved by 1% of the time
where the time goes in v8:
time: 18.9 us; the launch traced here: 18.7 us
  Pallas kernels  18.7 us (99%)
    pallas_call x1, Pallas kernels, local(): pl.pallas_call(functools.partial(kernel, n, reach, 512), out_shape=(pltpu...  17.4 us
    pallas_call x1, Pallas kernels, local(): pl.pallas_call(functools.partial(finish_kernel, n, tree, 512), out_shape=...  1.33 us

profile of v8, /device:TPU:13, one launch (start us, length us, event | category | flops | bytes accessed | tf_op | source)
XLA Modules:
  0.0 18.7 jit_solution(8902932274589130228)
XLA Ops:
  0.0 17.4 %shard_map.55 = (bf16[128,8,8,128]{3,2,1,0:T(8,128)(2,1)S(1)}, bf16[1024,512]{1,0:T(8,128)(2,1)S(1)}, f32[8,1024,128]{2,1,0:T(8,128)S(1)}, f32[8,1024,128]{2,1,0...) custom-call(s32[8]{0:T(128)} %counts_hbm.1, bf16[128,8,8,128]{3,2,1,0:T(8,128)(2,1)} %bitcast.3, ...), custom_call_target="tpu_custom_call" | custom-call | tf_op jit(solution)/shard_map/pallas_call | solution.py:441
  17.4 1.3 %shard_map.56 = bf16[128,8,8,128]{3,2,1,0:T(8,128)(2,1)} custom-call(bf16[128,8,8,128]{3,2,1,0:T(8,128)(2,1)S(1)} %get-tuple-element.11.mixed_ref, bf16[1024,512]{1,0:T(8,128)(2,1)S(1)} %get-tuple-element.12.weights, f32[8,1024,128]{2,1,0:T(8,128)S(1)} %get-tuple-element.13.top_ref, f32[8,1024,128]{2,1,0:T(8,128)S(1)} %get-tuple-element.14.norm_ref, ...), custom_call_target="tpu_custom_call" | custom-call | tf_op jit(solution)/shard_map/pallas_call | solution.py:484
